TPU v7x, 256 devices: a whole 4x4x8 slice. The times are simulated.
256 devices in a mesh: dp: 256 (over y, z, x, core).
Axes of the slice: x: 4, y: 4, z: 8, core: 2. Of those that a mesh axis runs over, the one named last changes fastest.
Arguments:
- features: bfloat16 [512, 256, 256], P('dp'), may hold values from -6 to 6
- frame_lens: int32 [512], P('dp'), may hold values from 128 to 256
- labels: int32 [512, 48], P('dp'), may hold values from 1 to 255
- label_lens: int32 [512], P('dp'), may hold values from 1 to 48
- w_up: float32 [262144], P('dp'), may hold values from -0.375 to 0.375
- w_down: float32 [262144], P('dp'), may hold values from -0.1875 to 0.1875
- w_out: float32 [65536], P('dp'), may hold values from -1.125 to 1.125
- first_up: float32 [262144], P('dp'), may hold values from -0.00018 to 0.00018
- first_down: float32 [262144], P('dp'), may hold values from -0.00018 to 0.00018
- first_out: float32 [65536], P('dp'), may hold values from -0.00018 to 0.00018
- second_up: float32 [262144], P('dp'), may hold values from 1e-10 to 1e-08
- second_down: float32 [262144], P('dp'), may hold values from 1e-10 to 1e-08
- second_out: float32 [65536], P('dp'), may hold values from 1e-10 to 1e-08
Outputs:
- new_up: float32 [262144], P('dp')
- new_down: float32 [262144], P('dp')
- new_out: float32 [65536], P('dp')
- new_first_up: float32 [262144], P('dp')
- new_first_down: float32 [262144], P('dp')
- new_first_out: float32 [65536], P('dp')
- new_second_up: float32 [262144], P('dp')
- new_second_down: float32 [262144], P('dp')
- new_second_out: float32 [65536], P('dp')
Inputs may be any that keep to these rules, and one draw needn't show every extreme that they name: `labels`: 0 is the blank and is not a label.
All inputs are finite; a program needn't handle non-finite values.
Results may differ from a plain program's by a relative error of at most 0.002.
The roundings to bfloat16 on the way count: a program that leaves them out, or rounds other values in their place, can miss the bound.
Values may be sent and summed in bfloat16 or wider, within the bound.
No kernel may reach another device: no remote copies, remote signals or barrier semaphores. Data moves between devices by JAX's collectives and lax.ppermute only.
A program may use at most 64 MiB of HBM per device.

v0:
```python
import math

import jax
import jax.numpy as jnp
from jax import lax
from jax.sharding import Mesh
from jax.sharding import PartitionSpec as P

D = 256
FF = 1024
VOCAB = 256
UTT = 2
DP = ("dp_0", "dp_1", "dp_2", "dp_3")


first_correction = 1.0 - (0.9**10) ** 10
second_correction = 1.0 - (0.999**10) ** 10
negative = -1e30


def sent_to_all(value, axis):
    copies = jnp.broadcast_to(value, (lax.axis_size(axis), *value.shape))
    return lax.all_to_all(copies, axis, split_axis=0, concat_axis=0, tiled=True)


def of_everyone(value, axis):
    return sent_to_all(value, axis).sum(axis=0)


def over_axes(value, axes):
    far, near = axes
    nearer = of_everyone(value, near)
    return of_everyone(nearer, far)


def in_order(blocks, dim):
    lengths = list(blocks.shape[1:])
    lengths[dim] *= blocks.shape[0]
    return jnp.moveaxis(blocks, 0, dim).reshape(lengths)


def whole_of(value, axes, dim):
    far, near = axes
    first = sent_to_all(value, far)
    blocks = jnp.swapaxes(sent_to_all(first, near), 0, 1)
    return in_order(blocks.reshape(-1, *value.shape), dim)


def cut_along(value, dim, size):
    lengths = value.shape
    blocks = value.reshape(*lengths[:dim], size, lengths[dim] // size, *lengths[dim + 1 :])
    return jnp.moveaxis(blocks, dim, 0)


def summed_on_arrival(value, axis, dim):
    size = lax.axis_size(axis)
    blocks = lax.all_to_all(cut_along(value, dim, size), axis, 0, 0, tiled=True)
    return jnp.sum(blocks, axis=0)


def sum_by_axis(value, axes, dim):
    far, near = axes
    own = summed_on_arrival(cut_along(value, dim, lax.axis_size(far)), near, dim + 1)
    return jnp.sum(lax.all_to_all(own, far, 0, 0, tiled=True), axis=0)


def log_three(term_one, term_two, term_three):
    largest = jnp.maximum(jnp.maximum(term_one, term_two), term_three)
    return largest + jnp.log(
        jnp.exp(term_one - largest) + jnp.exp(term_two - largest) + jnp.exp(term_three - largest)
    )


def log_total(values, axis):
    largest = jnp.max(values, axis=axis, keepdims=True)
    return jnp.squeeze(largest, axis) + jnp.log(jnp.sum(jnp.exp(values - largest), axis=axis))


def skew_behind(table_in):
    leading = table_in.shape[:-2]
    band_size, states = (table_in.shape[-2], table_in.shape[-1])
    row_length = states + band_size
    padded = jnp.pad(
        table_in, [(0, 0)] * len(leading) + [(0, 0), (band_size, 0)], constant_values=negative
    )
    flattened = padded.reshape(leading + (band_size * row_length,))
    retained = lax.slice_in_dim(
        flattened, band_size, band_size + band_size * (row_length - 1), axis=len(leading)
    )
    return retained.reshape(leading + (band_size, row_length - 1))[..., :states]


def skew_ahead(table_in):
    leading = table_in.shape[:-2]
    band_size, states = (table_in.shape[-2], table_in.shape[-1])
    row_length = states + band_size
    padded = jnp.pad(
        table_in, [(0, 0)] * len(leading) + [(0, 0), (0, band_size)], constant_values=negative
    )
    flattened = padded.reshape(leading + (band_size * row_length,))
    lengthened = jnp.pad(
        flattened, [(0, 0)] * len(leading) + [(0, band_size)], constant_values=negative
    )
    return lengthened.reshape(leading + (band_size, row_length + 1))[..., :states]


def ctc_logit_grad(log_probs, labels, frame_lens, label_lens, loss_scale):
    batch, frames, vocab = log_probs.shape
    label_count = labels.shape[1]
    states = 2 * label_count + 1
    padded_states = (states + 127) // 128 * 128
    frame_block = math.gcd(frames, 1 << (frames.bit_length() - 1) // 2)
    blocks = frames // frame_block
    band_size = 2 * frame_block + 1
    blanks = jnp.zeros_like(labels)
    extended = jnp.concatenate(
        [jnp.stack([blanks, labels], axis=2).reshape(batch, 2 * label_count), blanks[:, :1]], axis=1
    )
    extended = jnp.pad(extended, ((0, 0), (0, padded_states - states)))
    earlier = jnp.concatenate([jnp.full((batch, 2), -1, jnp.int32), extended[:, :-2]], axis=1)
    may_skip = (extended != 0) & (extended != earlier)
    skip_later = jnp.pad(may_skip[:, 2:], ((0, 0), (0, 2)))
    state_ids = jnp.arange(padded_states, dtype=jnp.int32)
    valid_state = state_ids < states
    onehot = (
        (extended[:, :, None] == jnp.arange(vocab, dtype=jnp.int32)[None, None, :])
        & valid_state[None, :, None]
    ).astype(jnp.float32)
    picked = jnp.einsum("btv,bsv->bts", log_probs, onehot, precision=lax.Precision.HIGHEST)
    emitted = jnp.where(valid_state[None, None, :], picked, negative)
    frame_ids = jnp.arange(frames, dtype=jnp.int32)
    alive = frame_ids[None, :] < frame_lens[:, None]
    emit_blocks = emitted.reshape(batch, blocks, frame_block, padded_states).transpose(2, 1, 0, 3)
    alive_blocks = alive.reshape(batch, blocks, frame_block).transpose(2, 1, 0)
    offsets = jnp.arange(band_size, dtype=jnp.int32)
    identity_row = jnp.where(offsets[:, None] == 0, 0.0, negative).astype(jnp.float32)
    identity = jnp.broadcast_to(
        identity_row[None, None, :, :], (blocks, batch, band_size, padded_states)
    )
    skip_grid = may_skip[None, :, None, :]

    def extend_band(transfer, inputs):
        emit_rows, live = inputs
        shifted = jnp.pad(transfer, ((0, 0), (0, 0), (2, 0), (2, 0)), constant_values=negative)
        from_one = shifted[:, :, 1 : band_size + 1, 1 : padded_states + 1]
        from_two = jnp.where(skip_grid, shifted[:, :, :band_size, :padded_states], negative)
        merged = log_three(transfer, from_one, from_two) + emit_rows[:, :, None, :]
        return (jnp.where(live[:, :, None, None], merged, transfer), None)

    transfers, _ = lax.scan(extend_band, identity, (emit_blocks, alive_blocks))
    start = jnp.broadcast_to(
        jnp.where(state_ids == 0, 0.0, negative).astype(jnp.float32)[None, :],
        (batch, padded_states),
    )
    last_state = 2 * label_lens
    at_end = (state_ids[None, :] == last_state[:, None]) | (
        state_ids[None, :] == last_state[:, None] - 1
    )
    finish = jnp.where(at_end, 0.0, negative).astype(jnp.float32)

    def cross_blocks(carry, inputs):
        alpha_in, beta_out = carry
        forward_table, backward_table = inputs
        moved = (
            skew_behind(jnp.broadcast_to(alpha_in[:, None, :], forward_table.shape)) + forward_table
        )
        alpha_next = log_total(moved, 1)
        returned = skew_ahead(backward_table + beta_out[:, None, :])
        beta_prev = log_total(returned, 1)
        return ((alpha_next, beta_prev), (alpha_in, beta_out))

    (alpha_final, _), (alpha_starts, beta_reversed) = lax.scan(
        cross_blocks, (start, finish), (transfers, transfers[::-1])
    )
    beta_ends = beta_reversed[::-1]
    log_total_prob = log_total(alpha_final + finish, 1)

    def inside_block(carry, inputs):
        alpha_now, beta_now = carry
        emit_forward, live_forward, emit_backward, live_backward = inputs
        alpha_pad = jnp.pad(alpha_now, ((0, 0), (0, 0), (2, 0)), constant_values=negative)
        alpha_skip = jnp.where(may_skip[None], alpha_pad[..., :padded_states], negative)
        alpha_new = (
            log_three(alpha_now, alpha_pad[..., 1 : padded_states + 1], alpha_skip) + emit_forward
        )
        alpha_new = jnp.where(live_forward[..., None], alpha_new, alpha_now)
        weighted = beta_now + emit_backward
        weighted_pad = jnp.pad(weighted, ((0, 0), (0, 0), (0, 2)), constant_values=negative)
        beta_skip = jnp.where(skip_later[None], weighted_pad[..., 2 : padded_states + 2], negative)
        beta_new = log_three(weighted, weighted_pad[..., 1 : padded_states + 1], beta_skip)
        beta_new = jnp.where(live_backward[..., None], beta_new, beta_now)
        return ((alpha_new, beta_new), (alpha_new, beta_now))

    _, (alpha_rows, beta_rows) = lax.scan(
        inside_block,
        (alpha_starts, beta_ends),
        (emit_blocks, alive_blocks, emit_blocks[::-1], alive_blocks[::-1]),
    )
    alpha_all = alpha_rows.transpose(2, 1, 0, 3).reshape(batch, frames, padded_states)
    beta_all = beta_rows[::-1].transpose(2, 1, 0, 3).reshape(batch, frames, padded_states)
    occupancy = jnp.exp(alpha_all + beta_all - log_total_prob[:, None, None]) * alive[
        :, :, None
    ].astype(jnp.float32)
    gamma = jnp.einsum("bts,bsv->btv", occupancy, onehot, precision=lax.Precision.HIGHEST)
    probs = jnp.exp(log_probs)
    return loss_scale * (probs * jnp.sum(gamma, axis=-1, keepdims=True) - gamma)


def adam_update(weight, first, second, grad, clip):
    scaled = clip * grad
    new_first = 0.9 * first + 0.1 * scaled
    new_second = 0.999 * second + 0.001 * scaled * scaled
    ratio = new_first / first_correction / (jnp.sqrt(new_second / second_correction) + 1e-08)
    return (weight - 0.001 * ratio, new_first, new_second)


def squares_of(pieces):
    return (
        jnp.sum(pieces[0] * pieces[0])
        + jnp.sum(pieces[1] * pieces[1])
        + jnp.sum(pieces[2] * pieces[2])
    )


def global_squares(pieces):
    return over_axes(squares_of(pieces), (("dp_0", "dp_1"), ("dp_2", "dp_3")))


def per_device(
    features,
    frame_lens,
    labels,
    label_lens,
    w_up,
    w_down,
    w_out,
    first_up,
    first_down,
    first_out,
    second_up,
    second_down,
    second_out,
):
    devices = lax.axis_size(DP)
    batch, frames, width = features.shape
    full_up, full_down, full_out = (
        whole_of(w_up.astype(jnp.bfloat16), (("dp_0", "dp_1"), ("dp_2", "dp_3")), 0),
        whole_of(w_down.astype(jnp.bfloat16), (("dp_0", "dp_1"), ("dp_2", "dp_3")), 0),
        whole_of(w_out.astype(jnp.bfloat16), (("dp_0", "dp_1"), ("dp_2", "dp_3")), 0),
    )
    up_mat = full_up.reshape(D, FF)
    down_mat = full_down.reshape(FF, D)
    out_mat = full_out.reshape(D, VOCAB)
    loss_scale = 1.0 / (UTT * devices)
    flat_in = features.reshape(batch * frames, width).astype(jnp.float32)
    centre = jnp.mean(flat_in, axis=1, keepdims=True)
    spread = jnp.mean((flat_in - centre) ** 2, axis=1, keepdims=True)
    normalized = ((flat_in - centre) * lax.rsqrt(spread + 1e-05)).astype(jnp.bfloat16)
    activation = jnp.dot(normalized, up_mat, preferred_element_type=jnp.float32)
    hidden = jax.nn.silu(activation).astype(jnp.bfloat16)
    block_out = (
        flat_in + 0.5 * jnp.dot(hidden, down_mat, preferred_element_type=jnp.float32)
    ).astype(jnp.bfloat16)
    logits = jnp.dot(block_out, out_mat, preferred_element_type=jnp.float32)
    log_probs = jax.nn.log_softmax(logits.reshape(batch, frames, VOCAB), axis=-1)
    logit_grad = ctc_logit_grad(log_probs, labels, frame_lens, label_lens, loss_scale)
    logit_grad = logit_grad.reshape(batch * frames, VOCAB).astype(jnp.bfloat16)
    grad_out = jnp.dot(block_out.T, logit_grad, preferred_element_type=jnp.float32).reshape(-1)
    ff_grad = (0.5 * jnp.dot(logit_grad, out_mat.T, preferred_element_type=jnp.float32)).astype(
        jnp.bfloat16
    )
    grad_down = jnp.dot(hidden.T, ff_grad, preferred_element_type=jnp.float32).reshape(-1)
    sigmoid = jax.nn.sigmoid(activation)
    slope = sigmoid * (1.0 + activation * (1.0 - sigmoid))
    act_grad = (jnp.dot(ff_grad, down_mat.T, preferred_element_type=jnp.float32) * slope).astype(
        jnp.bfloat16
    )
    grad_up = jnp.dot(normalized.T, act_grad, preferred_element_type=jnp.float32).reshape(-1)
    share_up, share_down, share_out = (
        sum_by_axis(grad_up, (("dp_0", "dp_1"), ("dp_2", "dp_3")), 0),
        sum_by_axis(grad_down, (("dp_0", "dp_1"), ("dp_2", "dp_3")), 0),
        sum_by_axis(grad_out, (("dp_0", "dp_1"), ("dp_2", "dp_3")), 0),
    )
    total = global_squares((share_up, share_down, share_out))
    clip = 1.0 / jnp.maximum(jnp.sqrt(total), 1.0)
    new_up, new_first_up, new_second_up = adam_update(w_up, first_up, second_up, share_up, clip)
    new_down, new_first_down, new_second_down = adam_update(
        w_down, first_down, second_down, share_down, clip
    )
    new_out, new_first_out, new_second_out = adam_update(
        w_out, first_out, second_out, share_out, clip
    )
    return (
        new_up,
        new_down,
        new_out,
        new_first_up,
        new_first_down,
        new_first_out,
        new_second_up,
        new_second_down,
        new_second_out,
    )


def solution(mesh):
    finer = Mesh(mesh.devices.reshape(4, 8, 4, 2), ("dp_0", "dp_1", "dp_2", "dp_3"))
    return jax.shard_map(
        per_device,
        mesh=finer,
        in_specs=(
            P(DP, None, None),
            P(DP),
            P(DP, None),
            P(DP),
            P(DP),
            P(DP),
            P(DP),
            P(DP),
            P(DP),
            P(DP),
            P(DP),
            P(DP),
            P(DP),
        ),
        out_specs=(P(DP), P(DP), P(DP), P(DP), P(DP), P(DP), P(DP), P(DP), P(DP)),
        check_vma=False,
    )
```

profile of v0, /device:TPU:1, one launch (start us, length us, event | category | flops | bytes accessed | tf_op | source)
XLA Modules:
  0.0 312.1 jit_solution(3200173587692106630)
XLA Ops:
  3.2 12.0 %all-to-all-start.4 = ((bf16[32,2,128]{2,1,0:T(2,128)(2,1)}), bf16[32,2,128]{2,1,0:T(2,128)(2,1)S(1)}, u32[]{:S(2)}, u32[]{:S(2)}) async-start(bf16[32,2,128]{2,1,0:T(2,128)(2,1)} %reshape.213), calls=%async_computation.4 | async-start | bytes 32768 | tf_op jit(solution)/shard_map/all_to_all | solution.py:23
  22.0 1.9 all-to-all-done.4
  23.9 7.4 %all-to-all-start.2 = ((bf16[32,2,512]{2,1,0:T(2,128)(2,1)}), bf16[32,2,512]{2,1,0:T(2,128)(2,1)S(1)}, u32[]{:S(2)}, u32[]{:S(2)}) async-start(bf16[32,2,512]{2,1,0:T(2,128)(2,1)} %reshape.211), calls=%async_computation.2 | async-start | bytes 131072 | tf_op jit(solution)/shard_map/all_to_all | solution.py:23
  33.7 6.5 %all-to-all-done.2 = bf16[32,2,512]{2,1,0:T(2,128)(2,1)S(1)} async-done(((bf16[32,2,512]{2,1,0:T(2,128)(2,1)}), bf16[32,2,512]{2,1,0:T(2,128)(2,1)S(1)}, u32[]{:S(2)}, u32[]{:S(2)}) %all-to-all-start.2) | async-done | bytes 65568 | tf_op jit(solution)/shard_map/all_to_all | solution.py:23
  40.2 3.8 %all-to-all-start = ((bf16[32,2,512]{2,1,0:T(2,128)(2,1)}), bf16[32,2,512]{2,1,0:T(2,128)(2,1)S(1)}, u32[]{:S(2)}, u32[]{:S(2)}) async-start(bf16[32,2,512]{2,1,0:T(2,128)(2,1)} %reshape.209), calls=%async_computation | async-start | bytes 131072 | tf_op jit(solution)/shard_map/all_to_all | solution.py:23
  44.5 8.4 %all-to-all-done = bf16[32,2,512]{2,1,0:T(2,128)(2,1)S(1)} async-done(((bf16[32,2,512]{2,1,0:T(2,128)(2,1)}), bf16[32,2,512]{2,1,0:T(2,128)(2,1)S(1)}, u32[]{:S(2)}, u32[]{:S(2)}) %all-to-all-start) | async-done | bytes 65568 | tf_op jit(solution)/shard_map/all_to_all | solution.py:23
  53.8 8.1 %all-to-all-start.3 = ((bf16[8,32,1024]{2,1,0:T(8,128)(2,1)}), bf16[8,32,1024]{2,1,0:T(8,128)(2,1)S(1)}, u32[]{:S(2)}, u32[]{:S(2)}) async-start(bf16[8,32,1024]{2,1,0:T(8,128)(2,1)} %broadcast_in_dim.187), calls=%async_computation.3 | async-start | bytes 1048576 | tf_op jit(solution)/shard_map/all_to_all | solution.py:23
  63.1 8.1 %all-to-all-done.3 = bf16[8,32,1024]{2,1,0:T(8,128)(2,1)S(1)} async-done(((bf16[8,32,1024]{2,1,0:T(8,128)(2,1)}), bf16[8,32,1024]{2,1,0:T(8,128)(2,1)S(1)}, u32[]{:S(2)}, u32[]{:S(2)}) %all-to-all-start.3) | async-done | bytes 524320 | tf_op jit(solution)/shard_map/all_to_all | solution.py:23
  72.1 4.4 %all-to-all-start.1 = ((bf16[8,32,1024]{2,1,0:T(8,128)(2,1)}), bf16[8,32,1024]{2,1,0:T(8,128)(2,1)S(1)}, u32[]{:S(2)}, u32[]{:S(2)}) async-start(bf16[8,32,1024]{2,1,0:T(8,128)(2,1)} %broadcast_in_dim.185), calls=%async_computation.1 | async-start | bytes 1048576 | tf_op jit(solution)/shard_map/all_to_all | solution.py:23
  77.4 8.4 %all-to-all-done.1 = bf16[8,32,1024]{2,1,0:T(8,128)(2,1)S(1)} async-done(((bf16[8,32,1024]{2,1,0:T(8,128)(2,1)}), bf16[8,32,1024]{2,1,0:T(8,128)(2,1)S(1)}, u32[]{:S(2)}, u32[]{:S(2)}) %all-to-all-start.1) | async-done | bytes 524320 | tf_op jit(solution)/shard_map/all_to_all | solution.py:23
  86.5 4.2 %all-to-all-start.5 = ((bf16[8,32,256]{2,1,0:T(8,128)(2,1)}), bf16[8,32,256]{2,1,0:T(8,128)(2,1)S(1)}, u32[]{:S(2)}, u32[]{:S(2)}) async-start(bf16[8,32,256]{2,1,0:T(8,128)(2,1)} %broadcast_in_dim.189), calls=%async_computation.5 | async-start | bytes 262144 | tf_op jit(solution)/shard_map/all_to_all | solution.py:23
  90.7 2.1 multiply_convert_fusion.1
  94.3 1.7 all-to-all-done.5
  97.3 13.2 %while.42 = (s32[]{:T(128)}, f32[16,2,33,128]{3,2,1,0:T(8,128)S(1)}, pred[16,16,2]{1,2,0:T(4,128)(4,1)S(1)}, pred[1,2,1,128]{3,1,2,0:T(4,128)(4,1)S(1)}, f32[16,16,2,128]{3,2,1,0:T(2,128)S(1)}, /*index=5*/s32[]{:T(128)}) while((s32[]{:T(128)}, f32[16,2,33,128]{3,2,1,0:T(8,128)S(1)}, pred[16,16,2]{1,2,0:T(4,128)(4,1)S(1)}, ...), condition=%wide.region_5.6_spmd, body=%wide.region_4.5_spmd.sunk | while | flops 1486850 | bytes 2212341 | solution.py:150
  110.6 16.5 %while.43 = (s32[]{:T(128)}, f32[2,128]{1,0:T(2,128)S(1)}, f32[2,128]{1,0:T(2,128)S(1)}, f32[16,2,128]{2,1,0:T(2,128)S(1)}, f32[16,2,128]{2,1,0:T(2,128)S(1)}, /...) while((s32[]{:T(128)}, f32[2,128]{1,0:T(2,128)S(1)}, ...), condition=%wide.region_11.12_spmd, body=%wide.region_6.11_spmd.sunk | while | flops 75522 | bytes 985061 | solution.py:172
  127.1 60.8 %while.44 = (s32[]{:T(128)}, f32[16,2,128]{2,1,0:T(2,128)S(1)}, f32[16,2,128]{2,1,0:T(2,128)S(1)}, f32[16,16,2,128]{3,0,1,2:T(8,128)}, f32[16,16,2,128]{3,0,1,2:...) while((s32[]{:T(128)}, f32[16,2,128]{2,1,0:T(2,128)S(1)}, ...), condition=%wide.region_13.14_spmd, body=%wide.region_12.13_spmd.sunk | while | flops 90114 | bytes 312281 | solution.py:194
  127.7 1.6 dynamic_update_slice.20
  129.3 1.6 dynamic_update_slice.21
  131.5 1.6 dynamic_update_slice.20
  133.1 1.6 dynamic_update_slice.21
  135.3 1.6 dynamic_update_slice.20
  136.9 1.6 dynamic_update_slice.21
  139.1 1.6 dynamic_update_slice.20
  140.7 1.6 dynamic_update_slice.21
  142.9 1.6 dynamic_update_slice.20
  144.5 1.6 dynamic_update_slice.21
  146.7 1.6 dynamic_update_slice.20
  148.3 1.6 dynamic_update_slice.21
  150.5 1.6 dynamic_update_slice.20
  152.1 1.6 dynamic_update_slice.21
  154.3 1.6 dynamic_update_slice.20
  156.0 1.6 dynamic_update_slice.21
  158.1 1.6 dynamic_update_slice.20
  159.7 1.6 dynamic_update_slice.21
  161.9 1.6 dynamic_update_slice.20
  163.5 1.6 dynamic_update_slice.21
  165.7 1.6 dynamic_update_slice.20
  167.3 1.6 dynamic_update_slice.21
  169.5 1.6 dynamic_update_slice.20
  171.1 1.6 dynamic_update_slice.21
  173.3 1.6 dynamic_update_slice.20
  174.9 1.6 dynamic_update_slice.21
  177.1 1.6 dynamic_update_slice.20
  178.7 1.6 dynamic_update_slice.21
  180.9 1.6 dynamic_update_slice.20
  182.5 1.6 dynamic_update_slice.21
  184.7 1.6 dynamic_update_slice.20
  186.3 1.6 dynamic_update_slice.21
  193.0 4.2 %all-to-all-start.10 = ((f32[8,32,256]{2,1,0:T(8,128)}), f32[8,32,256]{2,1,0:T(8,128)S(1)}, u32[]{:S(2)}, u32[]{:S(2)}) async-start(f32[8,32,256]{2,1,0:T(8,128)} %copy.96), calls=%async_computation.10 | async-start | bytes 524288 | tf_op jit(solution)/shard_map/all_to_all | solution.py:57
  197.4 6.2 %all-to-all-done.10 = f32[8,32,256]{2,1,0:T(8,128)S(1)} async-done(((f32[8,32,256]{2,1,0:T(8,128)}), f32[8,32,256]{2,1,0:T(8,128)S(1)}, u32[]{:S(2)}, u32[]{:S(2)}) %all-to-all-start.10) | async-done | bytes 262176 | tf_op jit(solution)/shard_map/all_to_all | solution.py:57
  204.3 4.0 %all-to-all-start.11 = ((f32[32,1,256]{2,1,0:T(1,128)}), f32[32,1,256]{2,1,0:T(1,128)S(1)}, u32[]{:S(2)}, u32[]{:S(2)}) async-start(f32[32,1,256]{2,1,0:T(1,128)} %all_to_all.78), calls=%async_computation.11 | async-start | bytes 65536 | tf_op jit(solution)/shard_map/all_to_all | solution.py:64
  208.3 2.7 convolution_bitcast_fusion
  212.6 4.2 %all-to-all-done.11 = f32[32,1,256]{2,1,0:T(1,128)S(1)} async-done(((f32[32,1,256]{2,1,0:T(1,128)}), f32[32,1,256]{2,1,0:T(1,128)S(1)}, u32[]{:S(2)}, u32[]{:S(2)}) %all-to-all-start.11) | async-done | bytes 32800 | tf_op jit(solution)/shard_map/all_to_all | solution.py:64
  216.8 5.7 %all-to-all-start.6 = ((f32[8,32,1024]{2,1,0:T(8,128)}), f32[8,32,1024]{2,1,0:T(8,128)S(1)}, u32[]{:S(2)}, u32[]{:S(2)}) async-start(f32[8,32,1024]{2,1,0:T(8,128)} %copy.93), calls=%async_computation.6 | async-start | bytes 2097152 | tf_op jit(solution)/shard_map/all_to_all | solution.py:57
  223.2 1.6 copy.150
  224.9 12.6 %all-to-all-done.6 = f32[8,32,1024]{2,1,0:T(8,128)S(1)} async-done(((f32[8,32,1024]{2,1,0:T(8,128)}), f32[8,32,1024]{2,1,0:T(8,128)S(1)}, u32[]{:S(2)}, u32[]{:S(2)}) %all-to-all-start.6) | async-done | bytes 1048608 | tf_op jit(solution)/shard_map/all_to_all | solution.py:57
  237.4 4.4 %all-to-all-start.8 = ((f32[8,32,1024]{2,1,0:T(8,128)}), f32[8,32,1024]{2,1,0:T(8,128)S(1)}, u32[]{:S(2)}, u32[]{:S(2)}) async-start(f32[8,32,1024]{2,1,0:T(8,128)} %bitcast.116), calls=%async_computation.8 | async-start | bytes 2097152 | tf_op jit(solution)/shard_map/all_to_all | solution.py:57
  242.8 14.1 %all-to-all-done.8 = f32[8,32,1024]{2,1,0:T(8,128)S(1)} async-done(((f32[8,32,1024]{2,1,0:T(8,128)}), f32[8,32,1024]{2,1,0:T(8,128)S(1)}, u32[]{:S(2)}, u32[]{:S(2)}) %all-to-all-start.8) | async-done | bytes 1048608 | tf_op jit(solution)/shard_map/all_to_all | solution.py:57
  256.9 4.0 %all-to-all-start.7 = ((f32[32,1,1024]{2,1,0:T(1,128)}), f32[32,1,1024]{2,1,0:T(1,128)S(1)}, u32[]{:S(2)}, u32[]{:S(2)}) async-start(f32[32,1,1024]{2,1,0:T(1,128)} %all_to_all.72), calls=%async_computation.7 | async-start | bytes 262144 | tf_op jit(solution)/shard_map/all_to_all | solution.py:64
  261.7 8.4 %all-to-all-done.7 = f32[32,1,1024]{2,1,0:T(1,128)S(1)} async-done(((f32[32,1,1024]{2,1,0:T(1,128)}), f32[32,1,1024]{2,1,0:T(1,128)S(1)}, u32[]{:S(2)}, u32[]{:S(2)}) %all-to-all-start.7) | async-done | bytes 131104 | tf_op jit(solution)/shard_map/all_to_all | solution.py:64
  270.1 3.9 %all-to-all-start.9 = ((f32[32,1,1024]{2,1,0:T(1,128)}), f32[32,1,1024]{2,1,0:T(1,128)S(1)}, u32[]{:S(2)}, u32[]{:S(2)}) async-start(f32[32,1,1024]{2,1,0:T(1,128)} %all_to_all.75), calls=%async_computation.9 | async-start | bytes 262144 | tf_op jit(solution)/shard_map/all_to_all | solution.py:64
  275.3 7.8 %all-to-all-done.9 = f32[32,1,1024]{2,1,0:T(1,128)S(1)} async-done(((f32[32,1,1024]{2,1,0:T(1,128)}), f32[32,1,1024]{2,1,0:T(1,128)S(1)}, u32[]{:S(2)}, u32[]{:S(2)}) %all-to-all-start.9) | async-done | bytes 131104 | tf_op jit(solution)/shard_map/all_to_all | solution.py:64
  285.7 10.5 %all_to_all.96 = f32[8,1,1]{2,1,0:T(1,128)S(1)} all-to-all(f32[8,1,1]{2,1,0:T(1,128)S(1)} %broadcast_in_dim.201), channel_id=1, replica_groups=mesh['dp_0'=4,'dp_1'=8,'dp_2'=4,'dp_3'=2] {'dp_2','dp_3'}, dimensions={0} | all-to-all | bytes 64 | tf_op jit(solution)/shard_map/all_to_all | solution.py:23
  297.6 11.8 %all_to_all.97 = f32[32,1,1]{2,1,0:T(1,128)S(1)} all-to-all(f32[32,1,1]{2,1,0:T(1,128)S(1)} %broadcast_in_dim.202), channel_id=1, replica_groups=mesh['dp_0'=4,'dp_1'=8,'dp_2'=4,'dp_3'=2] {'dp_0','dp_1'}, dimensions={0} | all-to-all | bytes 256 | tf_op jit(solution)/shard_map/all_to_all | solution.py:23
  (613 shorter events, 70.4 us)
Async XLA Ops:
  0.6 43.4 %copy-start.13 = (s32[2,48]{1,0:T(2,128)S(1)}, s32[2,48]{1,0:T(2,128)}, u32[]{:S(2)}) copy-start(s32[2,48]{1,0:T(2,128)} %param.21) | copy-start | bytes 1156
  3.2 20.7 %all-to-all-start.4 = ((bf16[32,2,128]{2,1,0:T(2,128)(2,1)}), bf16[32,2,128]{2,1,0:T(2,128)(2,1)S(1)}, u32[]{:S(2)}, u32[]{:S(2)}) async-start(bf16[32,2,128]{2,1,0:T(2,128)(2,1)} %reshape.213), calls=%async_computation.4 | async-start | bytes 32768 | tf_op jit(solution)/shard_map/all_to_all | solution.py:23
  18.8 44.2 %copy-start.17 = (s32[2]{0:T(128)S(1)}, s32[2]{0:T(128)}, u32[]{:S(2)}) copy-start(s32[2]{0:T(128)} %param.22) | copy-start | bytes 28
  18.8 44.2 %copy-start.12 = (s32[2]{0:T(128)S(1)}, s32[2]{0:T(128)}, u32[]{:S(2)}) copy-start(s32[2]{0:T(128)} %param.20) | copy-start | bytes 28
  23.9 16.3 %all-to-all-start.2 = ((bf16[32,2,512]{2,1,0:T(2,128)(2,1)}), bf16[32,2,512]{2,1,0:T(2,128)(2,1)S(1)}, u32[]{:S(2)}, u32[]{:S(2)}) async-start(bf16[32,2,512]{2,1,0:T(2,128)(2,1)} %reshape.211), calls=%async_computation.2 | async-start | bytes 131072 | tf_op jit(solution)/shard_map/all_to_all | solution.py:23
  40.2 12.7 %all-to-all-start = ((bf16[32,2,512]{2,1,0:T(2,128)(2,1)}), bf16[32,2,512]{2,1,0:T(2,128)(2,1)S(1)}, u32[]{:S(2)}, u32[]{:S(2)}) async-start(bf16[32,2,512]{2,1,0:T(2,128)(2,1)} %reshape.209), calls=%async_computation | async-start | bytes 131072 | tf_op jit(solution)/shard_map/all_to_all | solution.py:23
  52.9 23.6 %copy-start = (bf16[2,256,256]{2,1,0:T(8,128)(2,1)S(1)}, bf16[2,256,256]{2,1,0:T(8,128)(2,1)}, u32[]{:S(2)}) copy-start(bf16[2,256,256]{2,1,0:T(8,128)(2,1)} %param.19) | copy-start | bytes 786436
  53.8 17.5 %all-to-all-start.3 = ((bf16[8,32,1024]{2,1,0:T(8,128)(2,1)}), bf16[8,32,1024]{2,1,0:T(8,128)(2,1)S(1)}, u32[]{:S(2)}, u32[]{:S(2)}) async-start(bf16[8,32,1024]{2,1,0:T(8,128)(2,1)} %broadcast_in_dim.187), calls=%async_computation.3 | async-start | bytes 1048576 | tf_op jit(solution)/shard_map/all_to_all | solution.py:23
  72.1 13.7 %all-to-all-start.1 = ((bf16[8,32,1024]{2,1,0:T(8,128)(2,1)}), bf16[8,32,1024]{2,1,0:T(8,128)(2,1)S(1)}, u32[]{:S(2)}, u32[]{:S(2)}) async-start(bf16[8,32,1024]{2,1,0:T(8,128)(2,1)} %broadcast_in_dim.185), calls=%async_computation.1 | async-start | bytes 1048576 | tf_op jit(solution)/shard_map/all_to_all | solution.py:23
  86.5 9.5 %all-to-all-start.5 = ((bf16[8,32,256]{2,1,0:T(8,128)(2,1)}), bf16[8,32,256]{2,1,0:T(8,128)(2,1)S(1)}, u32[]{:S(2)}, u32[]{:S(2)}) async-start(bf16[8,32,256]{2,1,0:T(8,128)(2,1)} %broadcast_in_dim.189), calls=%async_computation.5 | async-start | bytes 262144 | tf_op jit(solution)/shard_map/all_to_all | solution.py:23
  92.9 1.0 copy-start.1
  190.9 17.4 %copy-start.3 = (bf16[256,512]{1,0:T(8,128)(2,1)S(1)}, bf16[256,512]{1,0:T(8,128)(2,1)}, u32[]{:S(2)}) copy-start(bf16[256,512]{1,0:T(8,128)(2,1)} %copy.85) | copy-start | bytes 786436
  193.0 10.7 %all-to-all-start.10 = ((f32[8,32,256]{2,1,0:T(8,128)}), f32[8,32,256]{2,1,0:T(8,128)S(1)}, u32[]{:S(2)}, u32[]{:S(2)}) async-start(f32[8,32,256]{2,1,0:T(8,128)} %copy.96), calls=%async_computation.10 | async-start | bytes 524288 | tf_op jit(solution)/shard_map/all_to_all | solution.py:57
  204.3 12.5 %all-to-all-start.11 = ((f32[32,1,256]{2,1,0:T(1,128)}), f32[32,1,256]{2,1,0:T(1,128)S(1)}, u32[]{:S(2)}, u32[]{:S(2)}) async-start(f32[32,1,256]{2,1,0:T(1,128)} %all_to_all.78), calls=%async_computation.11 | async-start | bytes 65536 | tf_op jit(solution)/shard_map/all_to_all | solution.py:64
  211.0 11.4 %copy-start.2 = (bf16[512,1024]{1,0:T(8,128)(2,1)S(1)}, bf16[512,1024]{1,0:T(8,128)(2,1)}, u32[]{:S(2)}) copy-start(bf16[512,1024]{1,0:T(8,128)(2,1)} %copy-done.1) | copy-start | bytes 3145732
  216.8 6.1 %copy-start.4 = (f32[32,1,256]{2,1,0:T(1,128)}, f32[32,1,256]{2,1,0:T(1,128)S(1)}, u32[]{:S(2)}) copy-start(f32[32,1,256]{2,1,0:T(1,128)S(1)} %all-to-all-done.11) | copy-start | bytes 98308
  216.8 20.7 %all-to-all-start.6 = ((f32[8,32,1024]{2,1,0:T(8,128)}), f32[8,32,1024]{2,1,0:T(8,128)S(1)}, u32[]{:S(2)}, u32[]{:S(2)}) async-start(f32[8,32,1024]{2,1,0:T(8,128)} %copy.93), calls=%async_computation.6 | async-start | bytes 2097152 | tf_op jit(solution)/shard_map/all_to_all | solution.py:57
  237.4 19.4 %all-to-all-start.8 = ((f32[8,32,1024]{2,1,0:T(8,128)}), f32[8,32,1024]{2,1,0:T(8,128)S(1)}, u32[]{:S(2)}, u32[]{:S(2)}) async-start(f32[8,32,1024]{2,1,0:T(8,128)} %bitcast.116), calls=%async_computation.8 | async-start | bytes 2097152 | tf_op jit(solution)/shard_map/all_to_all | solution.py:57
  241.9 32.1 %copy-start.5 = (f32[32,1,256]{2,1,0:T(1,128)S(1)}, f32[32,1,256]{2,1,0:T(1,128)}, u32[]{:S(2)}) copy-start(f32[32,1,256]{2,1,0:T(1,128)} %copy-done.4) | copy-start | bytes 98308
  241.9 68.9 %copy-start.14 = (f32[256]{0:T(256)S(1)}, f32[256]{0:T(256)}, u32[]{:S(2)}) copy-start(f32[256]{0:T(256)} %param.25) | copy-start | bytes 3076
  241.9 68.9 %copy-start.15 = (f32[256]{0:T(256)S(1)}, f32[256]{0:T(256)}, u32[]{:S(2)}) copy-start(f32[256]{0:T(256)} %param.28) | copy-start | bytes 3076
  241.9 68.9 %copy-start.16 = (f32[256]{0:T(256)S(1)}, f32[256]{0:T(256)}, u32[]{:S(2)}) copy-start(f32[256]{0:T(256)} %param.31) | copy-start | bytes 3076
  241.9 69.5 %copy-start.6 = (f32[1024]{0:T(1024)S(1)}, f32[1024]{0:T(1024)}, u32[]{:S(2)}) copy-start(f32[1024]{0:T(1024)} %param.24) | copy-start | bytes 12292
  241.9 69.5 %copy-start.7 = (f32[1024]{0:T(1024)S(1)}, f32[1024]{0:T(1024)}, u32[]{:S(2)}) copy-start(f32[1024]{0:T(1024)} %param.23) | copy-start | bytes 12292
  241.9 69.5 %copy-start.8 = (f32[1024]{0:T(1024)S(1)}, f32[1024]{0:T(1024)}, u32[]{:S(2)}) copy-start(f32[1024]{0:T(1024)} %param.27) | copy-start | bytes 12292
  241.9 69.5 %copy-start.9 = (f32[1024]{0:T(1024)S(1)}, f32[1024]{0:T(1024)}, u32[]{:S(2)}) copy-start(f32[1024]{0:T(1024)} %param.30) | copy-start | bytes 12292
  241.9 69.5 %copy-start.10 = (f32[1024]{0:T(1024)S(1)}, f32[1024]{0:T(1024)}, u32[]{:S(2)}) copy-start(f32[1024]{0:T(1024)} %param.29) | copy-start | bytes 12292
  241.9 69.5 %copy-start.11 = (f32[1024]{0:T(1024)S(1)}, f32[1024]{0:T(1024)}, u32[]{:S(2)}) copy-start(f32[1024]{0:T(1024)} %param.26) | copy-start | bytes 12292
  256.9 13.2 %all-to-all-start.7 = ((f32[32,1,1024]{2,1,0:T(1,128)}), f32[32,1,1024]{2,1,0:T(1,128)S(1)}, u32[]{:S(2)}, u32[]{:S(2)}) async-start(f32[32,1,1024]{2,1,0:T(1,128)} %all_to_all.72), calls=%async_computation.7 | async-start | bytes 262144 | tf_op jit(solution)/shard_map/all_to_all | solution.py:64
  270.1 13.0 %all-to-all-start.9 = ((f32[32,1,1024]{2,1,0:T(1,128)}), f32[32,1,1024]{2,1,0:T(1,128)S(1)}, u32[]{:S(2)}, u32[]{:S(2)}) async-start(f32[32,1,1024]{2,1,0:T(1,128)} %all_to_all.75), calls=%async_computation.9 | async-start | bytes 262144 | tf_op jit(solution)/shard_map/all_to_all | solution.py:64
where the time goes:
time: 314 us; the launch traced here: 312 us
  waiting for transfers between devices  88.2 us (28%)
  local copies, waits for them, and re-layouts  87.6 us (28%)
  starting transfers between devices  66 us (21%)
  other arithmetic  33.3 us (11%)
  blocking collectives  22.4 us (7%)
  matrix products  7.72 us (2%)
  between operations  3.97 us (1%)
    dynamic_update_slice x64, local copies, waits for them, and re-layouts, ctc_logit_grad(): lax.scan(inside_block, (alpha_starts, beta_ends), (emit_blocks, alive_blo...  52.2 us
    all_to_all x6, starting transfers between devices, sent_to_all(): return lax.all_to_all(copies, axis, split_axis=0, concat_axis=0, tiled=True)  39.9 us
    all_to_all x6, waiting for transfers between devices, sent_to_all(): return lax.all_to_all(copies, axis, split_axis=0, concat_axis=0, tiled=True)  35 us
    all_to_all x3, waiting for transfers between devices, summed_on_arrival(): blocks = lax.all_to_all(cut_along(value, dim, size), axis, 0, 0, tiled=True)  32.9 us
    all_to_all x2, blocking collectives, sent_to_all(): return lax.all_to_all(copies, axis, split_axis=0, concat_axis=0, tiled=True)  22.4 us
    all_to_all x3, waiting for transfers between devices, sum_by_axis(): return jnp.sum(lax.all_to_all(own, far, 0, 0, tiled=True), axis=0)  20.3 us
    all_to_all x3, starting transfers between devices, summed_on_arrival(): blocks = lax.all_to_all(cut_along(value, dim, size), axis, 0, 0, tiled=True)  14.3 us
    all_to_all x3, starting transfers between devices, sum_by_axis(): return jnp.sum(lax.all_to_all(own, far, 0, 0, tiled=True), axis=0)  11.8 us
  transfers between devices with their start and end apart: 12, of which 12 were waited for; matrix products, arithmetic and copies ran while one was open for 7% of the time, Pallas kernels for 0%

commit v1 on v0

v1 whole, which is shorter than its diff:
```python
import functools
import math

import jax
import jax.numpy as jnp
from jax import lax
from jax.experimental import pallas as pl
from jax.experimental.pallas import tpu as pltpu
from jax.sharding import Mesh
from jax.sharding import PartitionSpec as P

D = 256
FF = 1024
VOCAB = 256
UTT = 2
FRAMES = 256
LABELS = 48
STATES = 2 * LABELS + 1
LANES = 128
SPAN = 8
BLOCKS = FRAMES // SPAN
BANDS = 2 * SPAN + 1
ROWS = UTT * BLOCKS
SHARE = 2304
LOG2E = math.log2(math.e)
negative = -1e30
first_correction = 1.0 - (0.9**10) ** 10
second_correction = 1.0 - (0.999**10) ** 10
f32 = jnp.float32
bf16 = jnp.bfloat16


def log_sum(terms):
    largest = functools.reduce(jnp.maximum, terms)
    parts = [jnp.exp2(term - largest) for term in terms]
    while len(parts) > 1:
        parts = [sum(parts[i : i + 2]) for i in range(0, len(parts), 2)]
    return largest + jnp.log(parts[0]) * LOG2E


def back(value, amount):
    return value if amount == 0 else pltpu.roll(value, LANES - amount, 1)


def ahead(value, amount):
    return value if amount == 0 else pltpu.roll(value, amount, 1)


def dot_nn(a, b):
    return lax.dot_general(a, b, (((1,), (0,)), ((), ())), preferred_element_type=f32)


def dot_nt(a, b):
    return lax.dot_general(a, b, (((1,), (1,)), ((), ())), preferred_element_type=f32)


def dot_tn(a, b):
    return lax.dot_general(a, b, (((0,), (0,)), ((), ())), preferred_element_type=f32)


def ctc_occupancy(lens, onehot_ref, skip_ref, logit_ref, emit_ref, skips, table, starts, ends, alphas, occ_ref):
    lane = lax.broadcasted_iota(jnp.int32, (1, LANES), 1)
    for u in range(UTT):
        for d in range(BANDS):
            skips[u, d] = back(jnp.broadcast_to(skip_ref[u : u + 1, :], (8, LANES)), d)

    for u in range(UTT):
        value = logit_ref[pl.ds(u * FRAMES, FRAMES), :]
        high = value.astype(bf16)
        rest = value - high.astype(f32)
        middle = rest.astype(bf16)
        low = (rest - middle.astype(f32)).astype(bf16)
        onehot = onehot_ref[u]
        picked = dot_nt(high, onehot) + (dot_nt(middle, onehot) + dot_nt(low, onehot))
        picked = jnp.where(lane < STATES, picked, negative)
        top = jnp.max(picked, axis=1, keepdims=True)
        emit_ref[u] = jnp.where(lane < STATES, (picked - top) * LOG2E, negative)

    def build(group, carry):
        u = group // (BLOCKS // 8)
        first_block = (group % (BLOCKS // 8)) * 8
        frames = lens[u]
        begin = (first_block + lax.broadcasted_iota(jnp.int32, (8, LANES), 0)) * SPAN
        band = [None] * BANDS
        for j in range(SPAN):
            emit = emit_ref[u, pl.ds(first_block * SPAN + j, 8, stride=SPAN), :]
            live = begin + j < frames
            for d in range(2 * j + 2, -1, -1):
                here = back(emit, d)
                if j == 0:
                    new = (here, here, here + skips[u, 2])[d]
                    old = 0.0 if d == 0 else negative
                else:
                    terms = []
                    if d <= 2 * j:
                        terms.append(band[d])
                    if 0 <= d - 1 <= 2 * j:
                        terms.append(band[d - 1])
                    if 0 <= d - 2 <= 2 * j:
                        terms.append(band[d - 2] + skips[u, d])
                    new = (log_sum(terms) if len(terms) > 1 else terms[0]) + here
                    old = negative if band[d] is None else band[d]
                band[d] = jnp.where(live, new, old)
        for d in range(BANDS):
            table[d, pl.ds(group * 8, 8), :] = band[d]
        return carry

    lax.fori_loop(0, ROWS // 8, build, 0)

    row = lax.broadcasted_iota(jnp.int32, (UTT, LANES), 0)
    state = lax.broadcasted_iota(jnp.int32, (UTT, LANES), 1)
    last = 2 * jnp.where(row == 0, lens[2], lens[3])
    alpha = jnp.where(state == 0, 0.0, negative).astype(f32)
    beta = jnp.where((state == last) | (state == last - 1), 0.0, negative).astype(f32)

    def cross(i, carry):
        alpha, beta = carry
        k = BLOCKS - 1 - i
        starts[pl.ds(i, UTT, stride=BLOCKS), :] = alpha
        ends[pl.ds(k, UTT, stride=BLOCKS), :] = beta
        moved = [ahead(table[d, pl.ds(i, UTT, stride=BLOCKS), :] + alpha, d) for d in range(BANDS)]
        returned = [table[d, pl.ds(k, UTT, stride=BLOCKS), :] + back(beta, d) for d in range(BANDS)]
        return log_sum(moved), log_sum(returned)

    lax.fori_loop(0, BLOCKS, cross, (alpha, beta))

    for u in range(UTT):
        rows = pl.ds(u * BLOCKS, BLOCKS)
        frames = lens[u]
        begin = lax.broadcasted_iota(jnp.int32, (BLOCKS, LANES), 0) * SPAN
        skip = skip_ref[u : u + 1, :]
        skip_later = skips[u, 2, 0:1, :]
        now = starts[rows, :]
        for j in range(SPAN):
            emit = emit_ref[u, pl.ds(j, BLOCKS, stride=SPAN), :]
            new = log_sum([now, ahead(now, 1), ahead(now, 2) + skip]) + emit
            now = jnp.where(begin + j < frames, new, now)
            alphas[j] = now
        now = ends[rows, :]
        for j in range(SPAN - 1, -1, -1):
            live = begin + j < frames
            both = alphas[j] + now
            weight = jnp.exp2(both - jnp.max(both, axis=1, keepdims=True))
            share = weight / jnp.sum(weight, axis=1, keepdims=True)
            occ_ref[u, pl.ds(j, BLOCKS, stride=SPAN), :] = jnp.where(live, share, 0.0)
            if j > 0:
                emit = emit_ref[u, pl.ds(j, BLOCKS, stride=SPAN), :]
                passed = now + emit
                new = log_sum([passed, back(passed, 1), back(passed, 2) + skip_later])
                now = jnp.where(live, new, now)


def step_kernel(
    lens, x_ref, w_ref, onehot_ref, skip_ref, grad_ref,
    normal_ref, hidden_ref, slope_ref, block_ref, logit_ref,
    emit_ref, skips, table, starts, ends, alphas, occ_ref, lgrad_ref, fgrad_ref, agrad_ref, *, scale,
):
    chunk = 128

    def forward(c, carry):
        rows = pl.ds(pl.multiple_of(c * chunk, chunk), chunk)
        x = x_ref[rows, :].astype(f32)
        centred = x - jnp.mean(x, axis=1, keepdims=True)
        spread = jnp.mean(centred * centred, axis=1, keepdims=True)
        normal = (centred * lax.rsqrt(spread + 1e-05)).astype(bf16)
        normal_ref[rows, :] = normal
        total = jnp.zeros((chunk, D), f32)
        for q in range(4):
            cols = slice(256 * q, 256 * (q + 1))
            act = dot_nn(normal, w_ref[:, cols])
            sig = 1.0 / (1.0 + jnp.exp(-act))
            hid = (act * sig).astype(bf16)
            hidden_ref[rows, cols] = hid
            slope_ref[rows, cols] = sig * (1.0 + act * (1.0 - sig))
            total = total + dot_nn(hid, w_ref[:, FF + 256 * q : FF + 256 * (q + 1)])
        block = (x + 0.5 * total).astype(bf16)
        block_ref[rows, :] = block
        logit_ref[rows, :] = dot_nn(block, w_ref[:, 2 * FF : SHARE])
        return carry

    lax.fori_loop(0, UTT * FRAMES // chunk, forward, 0)

    ctc_occupancy(lens, onehot_ref, skip_ref, logit_ref, emit_ref, skips, table, starts, ends, alphas, occ_ref)

    def backward(c, carry):
        rows = pl.ds(pl.multiple_of(c * chunk, chunk), chunk)
        u = c // (FRAMES // chunk)
        inside = (c % (FRAMES // chunk)) * chunk
        occ = occ_ref[u, pl.ds(pl.multiple_of(inside, chunk), chunk), :]
        high = occ.astype(bf16)
        low = (occ - high.astype(f32)).astype(bf16)
        onehot = onehot_ref[u]
        gamma = dot_nn(high, onehot) + dot_nn(low, onehot)
        value = logit_ref[rows, :]
        raised = jnp.exp(value - jnp.max(value, axis=1, keepdims=True))
        probs = raised / jnp.sum(raised, axis=1, keepdims=True)
        frame = inside + lax.broadcasted_iota(jnp.int32, (chunk, 1), 0)
        lgrad = jnp.where(frame < lens[u], scale * (probs - gamma), 0.0).astype(bf16)
        lgrad_ref[rows, :] = lgrad
        fgrad = (0.5 * dot_nt(lgrad, w_ref[:, 2 * FF : SHARE])).astype(bf16)
        fgrad_ref[rows, :] = fgrad
        for q in range(4):
            cols = slice(256 * q, 256 * (q + 1))
            back_act = dot_nt(fgrad, w_ref[:, FF + 256 * q : FF + 256 * (q + 1)])
            agrad_ref[rows, cols] = (back_act * slope_ref[rows, cols]).astype(bf16)
        return carry

    lax.fori_loop(0, UTT * FRAMES // chunk, backward, 0)

    kind = grad_ref.dtype
    grad_ref[:, 2 * FF : SHARE] = dot_tn(block_ref[...], lgrad_ref[...]).astype(kind)
    for q in range(4):
        cols = slice(256 * q, 256 * (q + 1))
        grad_ref[:, FF + 256 * q : FF + 256 * (q + 1)] = dot_tn(hidden_ref[:, cols], fgrad_ref[...]).astype(kind)
        grad_ref[:, cols] = dot_tn(normal_ref[...], agrad_ref[:, cols]).astype(kind)


def local_gradients(lens, x, weights, onehot, skip, scale):
    vmem = pl.BlockSpec(memory_space=pltpu.VMEM)
    n = UTT * FRAMES
    return pl.pallas_call(
        functools.partial(step_kernel, scale=scale),
        out_shape=jax.ShapeDtypeStruct((D, SHARE), bf16),
        in_specs=[pl.BlockSpec(memory_space=pltpu.SMEM), vmem, vmem, vmem, vmem],
        out_specs=vmem,
        scratch_shapes=[
            pltpu.VMEM((n, D), bf16),
            pltpu.VMEM((n, FF), bf16),
            pltpu.VMEM((n, FF), f32),
            pltpu.VMEM((n, D), bf16),
            pltpu.VMEM((n, VOCAB), f32),
            pltpu.VMEM((UTT, FRAMES, LANES), f32),
            pltpu.VMEM((UTT, BANDS, 8, LANES), f32),
            pltpu.VMEM((BANDS, ROWS, LANES), f32),
            pltpu.VMEM((ROWS, LANES), f32),
            pltpu.VMEM((ROWS, LANES), f32),
            pltpu.VMEM((SPAN, BLOCKS, LANES), f32),
            pltpu.VMEM((UTT, FRAMES, LANES), f32),
            pltpu.VMEM((n, VOCAB), bf16),
            pltpu.VMEM((n, D), bf16),
            pltpu.VMEM((n, FF), bf16),
        ],
        compiler_params=pltpu.CompilerParams(vmem_limit_bytes=40 * 1024 * 1024),
        name="local_gradients",
    )(lens, x, weights, onehot, skip)


def label_tables(labels):
    blanks = jnp.zeros_like(labels)
    extended = jnp.stack([blanks, labels], axis=2).reshape(UTT, 2 * LABELS)
    extended = jnp.pad(extended, ((0, 0), (0, LANES - 2 * LABELS)))
    earlier = jnp.pad(extended[:, :-2], ((0, 0), (2, 0)), constant_values=-1)
    skip = jnp.where((extended != 0) & (extended != earlier), 0.0, negative).astype(f32)
    valid = jnp.arange(LANES, dtype=jnp.int32) < STATES
    onehot = (extended[:, :, None] == jnp.arange(VOCAB, dtype=jnp.int32)[None, None, :]) & valid[None, :, None]
    return onehot.astype(bf16), skip


def sent_to_all(value, axis):
    copies = jnp.broadcast_to(value, (lax.axis_size(axis), *value.shape))
    return lax.all_to_all(copies, axis, split_axis=0, concat_axis=0, tiled=True)


def adam_update(weight, first, second, grad, clip):
    scaled = clip * grad
    new_first = 0.9 * first + 0.1 * scaled
    new_second = 0.999 * second + 0.001 * scaled * scaled
    ratio = new_first / first_correction / (jnp.sqrt(new_second / second_correction) + 1e-08)
    return (weight - 0.001 * ratio, new_first, new_second)


NEAR = ("x", "core")
FAR = ("y", "z")
ALL = ("y", "z", "x", "core")


def per_device(
    features, frame_lens, labels, label_lens, w_up, w_down, w_out,
    first_up, first_down, first_out, second_up, second_down, second_out,
):
    near, far = lax.axis_size(NEAR), lax.axis_size(FAR)
    up_cut = w_up.astype(bf16).reshape(D, 4).T.reshape(-1)
    packed = jnp.concatenate([up_cut, w_down.astype(bf16), w_out.astype(bf16)])
    weights = sent_to_all(packed, ALL).reshape(near * far, SHARE)
    onehot, skip = label_tables(labels)
    lens = jnp.concatenate([frame_lens, label_lens])
    x = features.reshape(UTT * FRAMES, D)
    grads = local_gradients(lens, x, weights, onehot, skip, 1.0 / (UTT * near * far))
    cut = grads.reshape(far, near, SHARE).swapaxes(0, 1)
    part = jnp.sum(lax.all_to_all(cut, NEAR, 0, 0, tiled=True).astype(f32), axis=0)
    share = jnp.sum(lax.all_to_all(part.astype(bf16), FAR, 0, 0, tiled=True).astype(f32), axis=0)
    squares = jnp.broadcast_to(jnp.sum(share * share), (LANES,))
    squares = jnp.sum(sent_to_all(squares, ALL)[:, 0])
    clip = 1.0 / jnp.maximum(jnp.sqrt(squares), 1.0)
    g_up = share[:FF].reshape(4, D).T.reshape(-1)
    g_down = share[FF : 2 * FF]
    g_out = share[2 * FF :]
    up = adam_update(w_up, first_up, second_up, g_up, clip)
    down = adam_update(w_down, first_down, second_down, g_down, clip)
    out = adam_update(w_out, first_out, second_out, g_out, clip)
    return (up[0], down[0], out[0], up[1], down[1], out[1], up[2], down[2], out[2])


def solution(mesh):
    finer = Mesh(mesh.devices.reshape(4, 8, 4, 2), ALL)
    flat = P(ALL)
    return jax.shard_map(
        per_device,
        mesh=finer,
        in_specs=(P(ALL, None, None), flat, P(ALL, None)) + (flat,) * 10,
        out_specs=(flat,) * 9,
        check_vma=False,
    )
```

time: 314 us -> 147 us (0.47)
  local copies, waits for them, and re-layouts: 87.6 us -> 13 us
  waiting for transfers between devices: 88.2 us -> 32.4 us
  starting transfers between devices: 66 us -> 16.5 us
  blocking collectives: 22.4 us -> 53.1 us
  other arithmetic: 33.3 us -> 14.4 us
  Pallas kernels: 0 us -> 15.1 us
  matrix products: 7.72 us -> 0 us
    all_to_all x6 -> x0, waiting for transfers between devices: 53.2 us -> none  [the longest x3 32.9 us: summed_on_arrival(): blocks = lax.all_to_all(cut_along(value, dim, size), axis, 0, 0, tiled=True)]
    dynamic_update_slice x80 -> x0, local copies, waits for them, and re-layouts: 52.4 us -> none  [the longest x64 52.2 us: ctc_logit_grad(): lax.scan(inside_block, (alpha_starts, beta_ends), (emit_blocks, alive_blo...]
    all_to_all x0 -> x2, blocking collectives: none -> 33.2 us  [the longest x1 21 us: per_device(): lax.all_to_all(cut, NEAR, 0, 0, tiled=True).astype(f32)]
    all_to_all x6 -> x0, starting transfers between devices: 26.1 us -> none  [the longest x3 14.3 us: summed_on_arrival(): blocks = lax.all_to_all(cut_along(value, dim, size), axis, 0, 0, tiled=True)]
    all_to_all x6 -> x1, starting transfers between devices: 39.9 us -> 16.5 us  [sent_to_all(): return lax.all_to_all(copies, axis, split_axis=0, concat_axis=0, tiled=True)]
    pallas_call x0 -> x1, Pallas kernels: none -> 15.1 us  [local_gradients(): pl.pallas_call(functools.partial(step_kernel, scale=scale), out_shape=jax...]
    select_n x35 -> x1, other arithmetic: 12.4 us -> 0.08 us  [label_tables(): jnp.where((extended != 0) & (extended != earlier), 0.0, negative)]
    reshape x66 -> x3, local copies, waits for them, and re-layouts: 9.42 us -> 0.48 us  [the longest x1 0.19 us: per_device(): cut = grads.reshape(far, near, SHARE).swapaxes(0, 1)]
  transfers between devices with their start and end apart: 12 -> 1, of which waited for: 12 -> 1; matrix products, arithmetic and copies ran while one was open for 7% -> 0% of each run, Pallas kernels for 0% -> 0%
where the time goes in v1:
time: 147 us; the launch traced here: 146 us
  blocking collectives  53.1 us (36%)
  waiting for transfers between devices  32.4 us (22%)
  starting transfers between devices  16.5 us (11%)
  Pallas kernels  15.1 us (10%)
  other arithmetic  14.4 us (10%)
  local copies, waits for them, and re-layouts  13 us (9%)
  between operations  1.66 us (1%)
    all_to_all x1, waiting for transfers between devices, sent_to_all(): return lax.all_to_all(copies, axis, split_axis=0, concat_axis=0, tiled=True)  32.4 us
    all_to_all x1, blocking collectives, per_device(): lax.all_to_all(cut, NEAR, 0, 0, tiled=True).astype(f32)  21 us
    all_to_all x1, blocking collectives, sent_to_all(): return lax.all_to_all(copies, axis, split_axis=0, concat_axis=0, tiled=True)  19.9 us
    all_to_all x1, starting transfers between devices, sent_to_all(): return lax.all_to_all(copies, axis, split_axis=0, concat_axis=0, tiled=True)  16.5 us
    pallas_call x1, Pallas kernels, local_gradients(): pl.pallas_call(functools.partial(step_kernel, scale=scale), out_shape=jax...  15.1 us
    all_to_all x1, blocking collectives, per_device(): lax.all_to_all(part.astype(bf16), FAR, 0, 0, tiled=True).astype(f32)  12.2 us
    unnamed x33, local copies, waits for them, and re-layouts  9.65 us
    broadcast_in_dim x1, other arithmetic, sent_to_all(): copies = jnp.broadcast_to(value, (lax.axis_size(axis), *value.shape))  7.81 us
  transfers between devices with their start and end apart: 1, of which 1 were waited for; matrix products, arithmetic and copies ran while one was open for 0% of the time, Pallas kernels for 0%

profile of v1, /device:TPU:1, one launch (start us, length us, event | category | flops | bytes accessed | tf_op | source)
XLA Modules:
  0.0 146.2 jit_solution(4677701522035675011)
XLA Ops:
  0.6 0.7 convert_element_type.20
  1.3 0.7 convert_element_type.19
  2.0 0.7 convert_element_type.18
  2.7 0.2 reshape.62
  2.9 0.1 copy.42
  3.0 1.2 broadcast_in_dim.14
  4.2 0.5 broadcast.86
  4.7 7.8 %reduce.3 = bf16[256,2304]{1,0:T(8,128)(2,1)S(1)} reduce(bf16[256,1,2304]{2,1,0:T(2,128)(2,1)S(1)} %broadcast_in_dim.14, bf16[]{:T(256)} %broadcast.86), dimensions={1}, to_apply=%broadcast_in_dim.14.reduce_sub_computation | reduce | bytes 2359298 | tf_op jit(solution)/shard_map/broadcast_in_dim | solution.py:260
  12.5 1.2 reshape.66
  13.7 0.0 copy-start.7
  13.7 0.0 copy-start.11
  13.7 0.0 copy-start.12
  13.7 16.5 %all-to-all-start = ((bf16[256,2,1152]{2,1,0:T(2,128)(2,1)}), bf16[256,2,1152]{2,1,0:T(2,128)(2,1)}, u32[]{:S(2)}, u32[]{:S(2)}) async-start(bf16[256,2,1152]{2,1,0:T(2,128)(2,1)} %reshape.66), calls=%async_computation | async-start | bytes 2359296 | tf_op jit(solution)/shard_map/all_to_all | solution.py:261
  30.3 0.0 copy-done.7
  30.3 0.1 copy.50
  30.4 0.1 stack.7.clone
  30.5 0.1 reshape.64
  30.6 0.0 copy-done.11
  30.6 0.0 copy-done.12
  30.7 0.1 pad_add_fusion.lens
  30.7 0.1 and_select_fusion.skip_ref
  30.8 0.1 fusion.1.onehot_ref
  30.9 32.4 %all-to-all-done = bf16[256,2,1152]{2,1,0:T(2,128)(2,1)} async-done(((bf16[256,2,1152]{2,1,0:T(2,128)(2,1)}), bf16[256,2,1152]{2,1,0:T(2,128)(2,1)}, u32[]{:S(2)}, u32[]{:S(2)}) %all-to-all-start) | async-done | bytes 1179680 | tf_op jit(solution)/shard_map/all_to_all | solution.py:261
  63.4 7.2 %reshape.67 = bf16[256,1,2304]{2,1,0:T(2,128)(2,1)S(1)} reshape(bf16[256,2,1152]{2,1,0:T(2,128)(2,1)} %all-to-all-done) | data formatting | bytes 2359296
  70.6 0.0 copy-start
  70.6 0.1 copy.54
  70.7 0.8 copy-done
  71.5 15.1 %local_gradients.1 = bf16[256,2304]{1,0:T(8,128)(2,1)S(1)} custom-call(s32[4]{0:T(128)S(1)} %pad_add_fusion.lens, bf16[512,256]{1,0:T(8,128)(2,1)S(1)} %bitcast.17, bf16[256,2304]{1,0:T(8,128)(2,1)S(1)} %bitcast.15, bf16[2,128,256]{2,1,0:T(8,128)(2,1)S(1)} %fusion.1.onehot_ref, f32[2,128]{1,0:T(2,128)S(1)} %and_select_fusion.skip_ref), custom_call_target="tpu_custom_call" | custom-call | tf_op jit(solution)/shard_map/local_gradients/pallas_call | solution.py:221
  86.6 0.2 copy.55
  86.8 21.0 %all_to_all.31 = bf16[8,32,2304]{2,1,0:T(8,128)(2,1)S(1)} all-to-all(bf16[8,32,2304]{2,1,0:T(8,128)(2,1)S(1)} %bitcast.18), channel_id=1, replica_groups=mesh['y'=4,'z'=8,'x'=4,'core'=2] {'x','core'}, dimensions={0} | all-to-all | bytes 2359296 | tf_op jit(solution)/shard_map/all_to_all | solution.py:290
  107.8 0.2 reduce_sum.39
  107.9 0.0 copy-start.1
  108.0 0.0 copy-start.3
  108.0 0.0 copy-start.4
  108.0 0.0 copy-start.8
  108.0 0.0 copy-start.9
  108.0 0.0 copy-start.10
  108.0 0.7 reduce.4
  108.7 0.0 copy-start.2
  108.7 0.0 copy-start.5
  108.8 0.0 copy-start.6
  108.8 12.2 %all_to_all.32 = bf16[32,2,1152]{2,1,0:T(2,128)(2,1)S(1)} all-to-all(bf16[32,2,1152]{2,1,0:T(2,128)(2,1)S(1)} %reshape.68), channel_id=1, replica_groups=mesh['y'=4,'z'=8,'x'=4,'core'=2] {'y','z'}, dimensions={0} | all-to-all | bytes 294912 | tf_op jit(solution)/shard_map/all_to_all | solution.py:291
  121.0 0.1 reshape.69
  121.1 0.3 convert_reduce_fusion
  121.4 0.6 multiply_reduce_fusion
  122.0 0.7 broadcast_in_dim_broadcast_in_dim.3
  122.7 19.9 %all_to_all.33 = f32[256,1,128]{2,1,0:T(1,128)S(1)} all-to-all(f32[256,1,128]{2,1,0:T(1,128)S(1)} %broadcast_in_dim_broadcast_in_dim.3), channel_id=1, replica_groups=mesh['y'=4,'z'=8,'x'=4,'core'=2] {'y','z','x','core'}, dimensions={0} | all-to-all | bytes 262144 | tf_op jit(solution)/shard_map/all_to_all | solution.py:261
  142.6 0.6 slice_reduce_fusion
  144.0 0.0 copy-done.1
  144.0 0.0 copy-done.3
  144.0 0.0 copy-done.4
  144.0 0.6 multiply_subtract_fusion
  144.7 0.1 copy.47
  144.8 0.1 mul.97
  144.9 0.0 copy-done.8
  144.9 0.0 copy-done.9
  144.9 0.0 copy-done.10
  145.0 0.6 multiply_subtract_fusion.2
  145.5 0.0 copy-done.2
  145.5 0.0 copy-done.5
  145.5 0.0 copy-done.6
  145.6 0.6 multiply_subtract_fusion.1
  (7 shorter events, 0.1 us)
Async XLA Ops:
  13.7 16.5 %copy-start.7 = (s32[2,48]{1,0:T(2,128)S(1)}, s32[2,48]{1,0:T(2,128)}, u32[]{:S(2)}) copy-start(s32[2,48]{1,0:T(2,128)} %param.15) | copy-start | bytes 1156
  13.7 16.9 %copy-start.11 = (s32[2]{0:T(128)S(1)}, s32[2]{0:T(128)}, u32[]{:S(2)}) copy-start(s32[2]{0:T(128)} %param.16) | copy-start | bytes 28
  13.7 16.9 %copy-start.12 = (s32[2]{0:T(128)S(1)}, s32[2]{0:T(128)}, u32[]{:S(2)}) copy-start(s32[2]{0:T(128)} %param.14) | copy-start | bytes 28
  13.7 49.6 %all-to-all-start = ((bf16[256,2,1152]{2,1,0:T(2,128)(2,1)}), bf16[256,2,1152]{2,1,0:T(2,128)(2,1)}, u32[]{:S(2)}, u32[]{:S(2)}) async-start(bf16[256,2,1152]{2,1,0:T(2,128)(2,1)} %reshape.66), calls=%async_computation | async-start | bytes 2359296 | tf_op jit(solution)/shard_map/all_to_all | solution.py:261
  70.6 1.0 copy-start
  107.9 36.1 %copy-start.1 = (f32[1024]{0:T(1024)S(1)}, f32[1024]{0:T(1024)}, u32[]{:S(2)}) copy-start(f32[1024]{0:T(1024)} %param.18) | copy-start | bytes 12292
  108.0 36.1 %copy-start.3 = (f32[1024]{0:T(1024)S(1)}, f32[1024]{0:T(1024)}, u32[]{:S(2)}) copy-start(f32[1024]{0:T(1024)} %param.21) | copy-start | bytes 12292
  108.0 36.1 %copy-start.4 = (f32[1024]{0:T(1024)S(1)}, f32[1024]{0:T(1024)}, u32[]{:S(2)}) copy-start(f32[1024]{0:T(1024)} %param.24) | copy-start | bytes 12292
  108.0 36.9 %copy-start.8 = (f32[256]{0:T(256)S(1)}, f32[256]{0:T(256)}, u32[]{:S(2)}) copy-start(f32[256]{0:T(256)} %param.19) | copy-start | bytes 3076
  108.0 36.9 %copy-start.9 = (f32[256]{0:T(256)S(1)}, f32[256]{0:T(256)}, u32[]{:S(2)}) copy-start(f32[256]{0:T(256)} %param.22) | copy-start | bytes 3076
  108.0 36.9 %copy-start.10 = (f32[256]{0:T(256)S(1)}, f32[256]{0:T(256)}, u32[]{:S(2)}) copy-start(f32[256]{0:T(256)} %param.25) | copy-start | bytes 3076
  108.7 36.8 %copy-start.2 = (f32[1024]{0:T(1024)S(1)}, f32[1024]{0:T(1024)}, u32[]{:S(2)}) copy-start(f32[1024]{0:T(1024)} %param.17) | copy-start | bytes 12292
  108.7 36.8 %copy-start.5 = (f32[1024]{0:T(1024)S(1)}, f32[1024]{0:T(1024)}, u32[]{:S(2)}) copy-start(f32[1024]{0:T(1024)} %param.20) | copy-start | bytes 12292
  108.8 36.8 %copy-start.6 = (f32[1024]{0:T(1024)S(1)}, f32[1024]{0:T(1024)}, u32[]{:S(2)}) copy-start(f32[1024]{0:T(1024)} %param.23) | copy-start | bytes 12292

commit v2 on v1

--- a/solution.py
+++ b/solution.py
@@ -150,12 +150,27 @@
                 now = jnp.where(live, new, now)
 
 
+def order_of(place, shape, dim):
+    i = lax.broadcasted_iota(jnp.int32, shape, dim)
+    core = (i & 1) ^ place[1]
+    x = ((i >> 1) & 3) ^ place[0]
+    return core * 128 + x * 32 + (i >> 3)
+
+
 def step_kernel(
-    lens, x_ref, w_ref, onehot_ref, skip_ref, grad_ref,
-    normal_ref, hidden_ref, slope_ref, block_ref, logit_ref,
+    lens, place, x_ref, b0, b1, b2, b3, b4, b5, b6, b7, onehot_ref, skip_ref, keep_ref, send_ref,
+    w_ref, arrived_ref, normal_ref, hidden_ref, slope_ref, block_ref, logit_ref,
     emit_ref, skips, table, starts, ends, alphas, occ_ref, lgrad_ref, fgrad_ref, agrad_ref, *, scale,
 ):
     chunk = 128
+    for k, block in enumerate((b0, b1, b2, b3, b4, b5, b6, b7)):
+        arrived_ref[32 * k : 32 * (k + 1), :] = block[...]
+    square = (D, D)
+    gather = (order_of(place, square, 0) == lax.broadcasted_iota(jnp.int32, square, 1)).astype(f32).astype(bf16)
+    scatter = (order_of(place, square, 1) == lax.broadcasted_iota(jnp.int32, square, 0)).astype(f32).astype(bf16)
+    for q in range(9):
+        cols = slice(256 * q, 256 * (q + 1))
+        w_ref[:, cols] = dot_nn(gather, arrived_ref[:, cols]).astype(bf16)
 
     def forward(c, carry):
         rows = pl.ds(pl.multiple_of(c * chunk, chunk), chunk)
@@ -207,23 +222,30 @@
 
     lax.fori_loop(0, UTT * FRAMES // chunk, backward, 0)
 
-    kind = grad_ref.dtype
-    grad_ref[:, 2 * FF : SHARE] = dot_tn(block_ref[...], lgrad_ref[...]).astype(kind)
+    def put(cols, value):
+        moved = dot_nn(scatter, value.astype(bf16)).astype(bf16)
+        keep_ref[:, cols] = moved[:128]
+        send_ref[:, cols] = moved[128:]
+
+    put(slice(2 * FF, SHARE), dot_tn(block_ref[...], lgrad_ref[...]))
     for q in range(4):
         cols = slice(256 * q, 256 * (q + 1))
-        grad_ref[:, FF + 256 * q : FF + 256 * (q + 1)] = dot_tn(hidden_ref[:, cols], fgrad_ref[...]).astype(kind)
-        grad_ref[:, cols] = dot_tn(normal_ref[...], agrad_ref[:, cols]).astype(kind)
-
-
-def local_gradients(lens, x, weights, onehot, skip, scale):
+        put(slice(FF + 256 * q, FF + 256 * (q + 1)), dot_tn(hidden_ref[:, cols], fgrad_ref[...]))
+        put(cols, dot_tn(normal_ref[...], agrad_ref[:, cols]))
+
+
+def local_gradients(lens, place, x, blocks, onehot, skip, scale):
     vmem = pl.BlockSpec(memory_space=pltpu.VMEM)
+    smem = pl.BlockSpec(memory_space=pltpu.SMEM)
     n = UTT * FRAMES
     return pl.pallas_call(
         functools.partial(step_kernel, scale=scale),
-        out_shape=jax.ShapeDtypeStruct((D, SHARE), bf16),
-        in_specs=[pl.BlockSpec(memory_space=pltpu.SMEM), vmem, vmem, vmem, vmem],
-        out_specs=vmem,
+        out_shape=[jax.ShapeDtypeStruct((D // 2, SHARE), bf16)] * 2,
+        in_specs=[smem, smem] + [vmem] * 11,
+        out_specs=[vmem, vmem],
         scratch_shapes=[
+            pltpu.VMEM((D, SHARE), bf16),
+            pltpu.VMEM((D, SHARE), bf16),
             pltpu.VMEM((n, D), bf16),
             pltpu.VMEM((n, FF), bf16),
             pltpu.VMEM((n, FF), f32),
@@ -240,9 +262,9 @@
             pltpu.VMEM((n, D), bf16),
             pltpu.VMEM((n, FF), bf16),
         ],
-        compiler_params=pltpu.CompilerParams(vmem_limit_bytes=40 * 1024 * 1024),
+        compiler_params=pltpu.CompilerParams(vmem_limit_bytes=32 * 1024 * 1024),
         name="local_gradients",
-    )(lens, x, weights, onehot, skip)
+    )(lens, place, x, *blocks, onehot, skip)
 
 
 def label_tables(labels):
@@ -256,9 +278,28 @@
     return onehot.astype(bf16), skip
 
 
-def sent_to_all(value, axis):
-    copies = jnp.broadcast_to(value, (lax.axis_size(axis), *value.shape))
-    return lax.all_to_all(copies, axis, split_axis=0, concat_axis=0, tiled=True)
+def spread(shape):
+    lane = lax.broadcasted_iota(jnp.int32, shape, 0)
+    column = lax.broadcasted_iota(jnp.int32, shape, 1)
+    return (lane == 4 * (column % 32) + column // D).astype(f32)
+
+
+def own_rows(shape):
+    return (lax.broadcasted_iota(jnp.int32, shape, 1) % D) // 32 == lax.broadcasted_iota(jnp.int32, shape, 0)
+
+
+def pack_kernel(up_ref, down_ref, out_ref, packed_ref):
+    cut = dot_nn(up_ref[...].astype(bf16), spread((LANES, FF)).astype(bf16))
+    row = jnp.sum(jnp.where(own_rows((8, FF)), cut, 0.0), axis=0, keepdims=True)
+    packed_ref[:, :FF] = row
+    packed_ref[:, FF : 2 * FF] = down_ref[...].astype(bf16).astype(f32)
+    packed_ref[:, 2 * FF :] = out_ref[...].astype(bf16).astype(f32)
+
+
+def sum_kernel(arrived_ref, share_ref, square_ref):
+    share = jnp.sum(arrived_ref[...].astype(f32), axis=0, keepdims=True)
+    share_ref[...] = share
+    square_ref[...] = jnp.broadcast_to(jnp.sum(share * share, axis=1, keepdims=True), square_ref.shape)
 
 
 def adam_update(weight, first, second, grad, clip):
@@ -269,36 +310,75 @@
     return (weight - 0.001 * ratio, new_first, new_second)
 
 
-NEAR = ("x", "core")
+def adam_kernel(square_ref, share_ref, wu, wd, wo, fu, fd, fo, su, sd, so, *outs):
+    total = jnp.sum(square_ref[...], axis=0, keepdims=True)[:, :1]
+    clip = 1.0 / jnp.maximum(jnp.sqrt(total), 1.0)
+    placed = jnp.where(own_rows((8, FF)), jnp.broadcast_to(share_ref[:, :FF], (8, FF)), 0.0)
+    high = placed.astype(bf16)
+    rest = placed - high.astype(f32)
+    middle = rest.astype(bf16)
+    low = (rest - middle.astype(f32)).astype(bf16)
+    cut = spread((LANES, FF)).astype(bf16)
+    g_up = dot_nt(high, cut) + (dot_nt(middle, cut) + dot_nt(low, cut))
+    grads = (g_up, share_ref[:, FF : 2 * FF], share_ref[:, 2 * FF :])
+    for k, (w, m, v) in enumerate(((wu, fu, su), (wd, fd, sd), (wo, fo, so))):
+        new = adam_update(w[...], m[...], v[...], grads[k], clip)
+        for kind in range(3):
+            outs[3 * kind + k][...] = new[kind]
+
+
+def small_call(kernel, shapes, name, *args):
+    return pl.pallas_call(
+        kernel,
+        out_shape=[jax.ShapeDtypeStruct(s, f32) for s in shapes],
+        in_specs=[pl.BlockSpec(memory_space=pltpu.VMEM)] * len(args),
+        out_specs=[pl.BlockSpec(memory_space=pltpu.VMEM)] * len(shapes),
+        compiler_params=pltpu.CompilerParams(vmem_limit_bytes=8 * 1024 * 1024),
+        name=name,
+    )(*args)
+
+
 FAR = ("y", "z")
 ALL = ("y", "z", "x", "core")
+
+
+def swap_x(value, k):
+    return lax.ppermute(value, "x", [(i, i ^ k) for i in range(4)])
+
+
+def swap_core(value):
+    return lax.ppermute(value, "core", [(0, 1), (1, 0)])
 
 
 def per_device(
     features, frame_lens, labels, label_lens, w_up, w_down, w_out,
     first_up, first_down, first_out, second_up, second_down, second_out,
 ):
-    near, far = lax.axis_size(NEAR), lax.axis_size(FAR)
-    up_cut = w_up.astype(bf16).reshape(D, 4).T.reshape(-1)
-    packed = jnp.concatenate([up_cut, w_down.astype(bf16), w_out.astype(bf16)])
-    weights = sent_to_all(packed, ALL).reshape(near * far, SHARE)
+    far = lax.axis_size(FAR)
+    devices = lax.axis_size(ALL)
+    views = ((8, LANES), (1, FF), (1, D))
+    weights = [w.reshape(s) for w, s in zip((w_up, w_down, w_out), views)]
+    firsts = [w.reshape(s) for w, s in zip((first_up, first_down, first_out), views)]
+    seconds = [w.reshape(s) for w, s in zip((second_up, second_down, second_out), views)]
+    packed = small_call(pack_kernel, [(1, SHARE)], "pack", *weights)[0].astype(bf16)
+    copies = jnp.broadcast_to(packed.reshape(1, 2, SHARE // 2), (far, 2, SHARE // 2))
+    mine = lax.all_to_all(copies, FAR, 0, 0, tiled=True).reshape(far, SHARE)
+    same_core = [mine] + [swap_x(mine, k) for k in (1, 2, 3)]
+    blocks = same_core + [swap_core(block) for block in same_core]
     onehot, skip = label_tables(labels)
     lens = jnp.concatenate([frame_lens, label_lens])
+    place = jnp.stack([lax.axis_index("x"), lax.axis_index("core")]).astype(jnp.int32)
     x = features.reshape(UTT * FRAMES, D)
-    grads = local_gradients(lens, x, weights, onehot, skip, 1.0 / (UTT * near * far))
-    cut = grads.reshape(far, near, SHARE).swapaxes(0, 1)
-    part = jnp.sum(lax.all_to_all(cut, NEAR, 0, 0, tiled=True).astype(f32), axis=0)
-    share = jnp.sum(lax.all_to_all(part.astype(bf16), FAR, 0, 0, tiled=True).astype(f32), axis=0)
-    squares = jnp.broadcast_to(jnp.sum(share * share), (LANES,))
-    squares = jnp.sum(sent_to_all(squares, ALL)[:, 0])
-    clip = 1.0 / jnp.maximum(jnp.sqrt(squares), 1.0)
-    g_up = share[:FF].reshape(4, D).T.reshape(-1)
-    g_down = share[FF : 2 * FF]
-    g_out = share[2 * FF :]
-    up = adam_update(w_up, first_up, second_up, g_up, clip)
-    down = adam_update(w_down, first_down, second_down, g_down, clip)
-    out = adam_update(w_out, first_out, second_out, g_out, clip)
-    return (up[0], down[0], out[0], up[1], down[1], out[1], up[2], down[2], out[2])
+    keep, send = local_gradients(lens, place, x, blocks, onehot, skip, 1.0 / (UTT * devices))
+    part = keep.astype(f32) + swap_core(send).astype(f32)
+    parts = [part[32 * k : 32 * (k + 1)] for k in range(4)]
+    arrived = [swap_x(parts[k].astype(bf16), k).astype(f32) for k in (1, 2, 3)]
+    total = (parts[0] + arrived[0] + (arrived[1] + arrived[2])).astype(bf16)
+    summed = lax.all_to_all(total.reshape(far, 2, SHARE // 2), FAR, 0, 0, tiled=True).reshape(far, SHARE)
+    share, square = small_call(sum_kernel, [(1, SHARE), (devices, LANES)], "share", summed)
+    squares = lax.all_to_all(square, ALL, 0, 0, tiled=True)
+    outs = small_call(adam_kernel, list(views) * 3, "adam", squares, share, *weights, *firsts, *seconds)
+    return tuple(value.reshape(-1) for value in outs)
 
 
 def solution(mesh):

time: 147 us -> 104 us (0.71)
  blocking collectives: 53.1 us -> 34.4 us
  waiting for transfers between devices: 32.4 us -> 17 us
  other arithmetic: 14.4 us -> 1.32 us
  starting transfers between devices: 16.5 us -> 27.3 us
  local copies, waits for them, and re-layouts: 13 us -> 4.01 us
  Pallas kernels: 15.1 us -> 19 us
    all_to_all x1, waiting for transfers between devices: 32.4 us -> 8.15 us  [per_device(): mine = lax.all_to_all(copies, FAR, 0, 0, tiled=True).reshape(far, SHARE)]
    all_to_all x3 -> x2, blocking collectives: 53.1 us -> 34.4 us  [the longest x1 21.1 us: per_device(): squares = lax.all_to_all(square, ALL, 0, 0, tiled=True)]
    ppermute x0 -> x11, starting transfers between devices: none -> 15.2 us  [the longest x5 8.56 us: swap_core(): return lax.ppermute(value, 'core', [(0, 1), (1, 0)])]
    ppermute x0 -> x11, waiting for transfers between devices: none -> 8.82 us  [the longest x6 6.48 us: swap_x(): return lax.ppermute(value, 'x', [(i, i ^ k) for i in range(4)])]
    broadcast_in_dim x1 -> x0, other arithmetic: 7.81 us -> none  [sent_to_all(): copies = jnp.broadcast_to(value, (lax.axis_size(axis), *value.shape))]
    unnamed x33 -> x29, local copies, waits for them, and re-layouts: 9.65 us -> 2.96 us
    all_to_all x1, starting transfers between devices: 16.5 us -> 12 us  [per_device(): mine = lax.all_to_all(copies, FAR, 0, 0, tiled=True).reshape(far, SHARE)]
    pallas_call x1 -> x4, Pallas kernels: 15.1 us -> 19 us  [the longest x1 17.7 us: local_gradients(): pl.pallas_call(functools.partial(step_kernel, scale=scale), out_shape=[ja...]
  transfers between devices with their start and end apart: 1 -> 12, of which waited for: 1 -> 8; matrix products, arithmetic and copies ran while one was open for 0% -> 2% of each run, Pallas kernels for 0% -> 0%
where the time goes in v2:
time: 104 us
  blocking collectives  34.4 us (33%)
  starting transfers between devices  27.3 us (26%)
  Pallas kernels  19 us (18%)
  waiting for transfers between devices  17 us (16%)
  local copies, waits for them, and re-layouts  4.01 us (4%)
  other arithmetic  1.32 us (1%)
    all_to_all x1, blocking collectives, per_device(): squares = lax.all_to_all(square, ALL, 0, 0, tiled=True)  21.1 us
    pallas_call x1, Pallas kernels, local_gradients(): pl.pallas_call(functools.partial(step_kernel, scale=scale), out_shape=[ja...  17.7 us
    all_to_all x1, blocking collectives, per_device(): lax.all_to_all(total.reshape(far, 2, SHARE // 2), FAR, 0, 0, tiled=True)  13.3 us
    all_to_all x1, starting transfers between devices, per_device(): mine = lax.all_to_all(copies, FAR, 0, 0, tiled=True).reshape(far, SHARE)  12 us
    ppermute x5, starting transfers between devices, swap_core(): return lax.ppermute(value, 'core', [(0, 1), (1, 0)])  8.56 us
    all_to_all x1, waiting for transfers between devices, per_device(): mine = lax.all_to_all(copies, FAR, 0, 0, tiled=True).reshape(far, SHARE)  8.15 us
    ppermute x6, starting transfers between devices, swap_x(): return lax.ppermute(value, 'x', [(i, i ^ k) for i in range(4)])  6.68 us
    ppermute x6, waiting for transfers between devices, swap_x(): return lax.ppermute(value, 'x', [(i, i ^ k) for i in range(4)])  6.48 us
  transfers between devices with their start and end apart: 12, of which 8 were waited for; matrix products, arithmetic and copies ran while one was open for 2% of the time, Pallas kernels for 0%

profile of v2, /device:TPU:1, one launch (start us, length us, event | category | flops | bytes accessed | tf_op | source)
XLA Modules:
  0.0 103.9 jit_solution(11506564514327199398)
XLA Ops:
  0.6 0.0 copy-start
  0.7 0.0 copy-start.1
  0.7 0.7 copy-done.1
  1.4 0.7 copy-done.3
  2.1 0.7 copy-done.5
  2.7 0.2 pack.1
  3.0 0.7 broadcast_in_dim.19
  3.7 12.0 %all-to-all-start = ((bf16[32,2,1152]{2,1,0:T(2,128)(2,1)}), bf16[32,2,1152]{2,1,0:T(2,128)(2,1)S(1)}, u32[]{:S(2)}, u32[]{:S(2)}) async-start(bf16[32,2,1152]{2,1,0:T(2,128)(2,1)} %broadcast_in_dim.19), calls=%async_computation | async-start | bytes 294912 | tf_op jit(solution)/shard_map/all_to_all | solution.py:365
  15.8 0.8 copy.26
  16.5 0.1 stack.19.clone
  16.6 0.1 reshape.101
  16.8 0.1 fusion.3.onehot_ref
  16.9 8.2 %all-to-all-done = bf16[32,2,1152]{2,1,0:T(2,128)(2,1)S(1)} async-done(((bf16[32,2,1152]{2,1,0:T(2,128)(2,1)}), bf16[32,2,1152]{2,1,0:T(2,128)(2,1)S(1)}, u32[]{:S(2)}, u32[]{:S(2)}) %all-to-all-start) | async-done | bytes 147488 | tf_op jit(solution)/shard_map/all_to_all | solution.py:365
  25.1 2.6 %collective-permute-start.2 = (bf16[32,2304]{1,0:T(8,128)(2,1)S(1)}, bf16[32,2304]{1,0:T(8,128)(2,1)S(1)}, u32[]{:S(2)}, u32[]{:S(2)}) collective-permute-start(bf16[32,2304]{1,0:T(8,128)(2,1)S(1)} %bitcast.30), channel_id=1, source_target_pairs={{0,6},{2,4},{4,2},{6,0},{1,7},{3,5},{5,3},{7,1},{8,14},{10,12},{12... | collective-permute-start | bytes 442376 | tf_op jit(solution)/shard_map/ppermute | solution.py:346
  27.6 0.5 collective-permute-start.1
  28.2 0.3 collective-permute-start
  28.4 0.1 pad_add_fusion.1.place
  28.5 3.0 %collective-permute-start.3 = (bf16[32,2304]{1,0:T(8,128)(2,1)S(1)}, bf16[32,2304]{1,0:T(8,128)(2,1)S(1)}, u32[]{:S(2)}, u32[]{:S(2)}) collective-permute-start(bf16[32,2304]{1,0:T(8,128)(2,1)S(1)} %bitcast.33), channel_id=1, source_target_pairs={{0,1},{1,0},{2,3},{3,2},{4,5},{5,4},{6,7},{7,6},{8,9},{9,8},{10,11... | collective-permute-start | bytes 442376 | tf_op jit(solution)/shard_map/ppermute | solution.py:350
  31.5 0.3 collective-permute-done.2.b3
  31.8 3.6 %collective-permute-start.6 = (bf16[32,2304]{1,0:T(8,128)(2,1)S(1)}, bf16[32,2304]{1,0:T(8,128)(2,1)S(1)}, u32[]{:S(2)}, u32[]{:S(2)}) collective-permute-start(bf16[32,2304]{1,0:T(8,128)(2,1)S(1)} %collective-permute-done.2.b3), channel_id=1, source_target_pairs={{0,1},{1,0},{2,3},{3,2},{4,5},{5,4},{6,7},{7,6},{8,9},{9,8},{10,11... | collective-permute-start | bytes 442376 | tf_op jit(solution)/shard_map/ppermute | solution.py:350
  35.3 0.0 collective-permute-done.1.b2
  35.3 1.7 %collective-permute-start.5 = (bf16[32,2304]{1,0:T(8,128)(2,1)S(1)}, bf16[32,2304]{1,0:T(8,128)(2,1)S(1)}, u32[]{:S(2)}, u32[]{:S(2)}) collective-permute-start(bf16[32,2304]{1,0:T(8,128)(2,1)S(1)} %collective-permute-done.1.b2), channel_id=1, source_target_pairs={{0,1},{1,0},{2,3},{3,2},{4,5},{5,4},{6,7},{7,6},{8,9},{9,8},{10,11... | collective-permute-start | bytes 442376 | tf_op jit(solution)/shard_map/ppermute | solution.py:350
  37.0 0.0 collective-permute-done.b1
  37.0 0.0 collective-permute-start.4
  37.0 0.7 pad_add_fusion.lens
  37.8 0.1 and_select_fusion.skip_ref
  37.9 0.0 collective-permute-done.3.b4
  37.9 0.0 collective-permute-done.6.b7
  37.9 0.2 collective-permute-done.5.b6
  38.0 0.4 collective-permute-done.4.b5
  38.4 0.0 copy-done
  38.4 17.7 %local_gradients.1 = (bf16[128,2304]{1,0:T(8,128)(2,1)S(1)}, bf16[128,2304]{1,0:T(8,128)(2,1)S(1)}) custom-call(s32[4]{0:T(128)S(1)} %pad_add_fusion.lens, s32[2]{0:T(128)S(1)} %pad_add_fusion.1.place, bf16[512,256]{1,0:T(8,128)(2,1)S(1)} %bitcast.37, bf16[32,2304]{1,0:T(8,128)(2,1)S(1)} %bitcast.34, bf16[32,2304]{1,0:T(8,128)(2,1)S(1)} %collective-permute-done.b1, ...), custom_call_target="tpu_custom_call" | custom-call | tf_op jit(solution)/shard_map/local_gradients/pallas_call | solution.py:241
  56.2 0.3 collective-permute-start.7
  56.4 1.8 %collective-permute-done.7 = bf16[128,2304]{1,0:T(8,128)(2,1)S(1)} collective-permute-done((bf16[128,2304]{1,0:T(8,128)(2,1)S(1)}, bf16[128,2304]{1,0:T(8,128)(2,1)S(1)}, u32[]{:S(2)}, u32[]{:S(2)}) %collective-permute-start.7) | collective-permute-done | bytes 589856 | tf_op jit(solution)/shard_map/ppermute | solution.py:350
  58.2 0.2 fusion.4
  58.5 0.0 copy-start.2
  58.5 0.0 copy-start.4
  58.5 0.0 copy-start.6
  58.5 0.0 copy-start.7
  58.5 0.0 copy-start.8
  58.5 0.0 copy-start.9
  58.6 0.0 copy-start.10
  58.6 0.0 copy-start.11
  58.6 0.0 copy-start.12
  58.6 0.3 collective-permute-start.8
  58.9 1.9 %collective-permute-start.10 = (bf16[32,2304]{1,0:T(8,128)(2,1)S(1)}, bf16[32,2304]{1,0:T(8,128)(2,1)S(1)}, u32[]{:S(2)}, u32[]{:S(2)}) collective-permute-start(bf16[32,2304]{1,0:T(8,128)(2,1)S(1)} %get-tuple-element.38), channel_id=1, source_target_pairs={{0,6},{2,4},{4,2},{6,0},{1,7},{3,5},{5,3},{7,1},{8,14},{10,12},{12... | collective-permute-start | bytes 442376 | tf_op jit(solution)/shard_map/ppermute | solution.py:346
  60.7 1.2 %collective-permute-start.9 = (bf16[32,2304]{1,0:T(8,128)(2,1)S(1)}, bf16[32,2304]{1,0:T(8,128)(2,1)S(1)}, u32[]{:S(2)}, u32[]{:S(2)}) collective-permute-start(bf16[32,2304]{1,0:T(8,128)(2,1)S(1)} %get-tuple-element.39), channel_id=1, source_target_pairs={{0,4},{2,6},{4,0},{6,2},{1,5},{3,7},{5,1},{7,3},{8,12},{10,14},{12... | collective-permute-start | bytes 442376 | tf_op jit(solution)/shard_map/ppermute | solution.py:346
  61.9 1.9 %collective-permute-done.8 = bf16[32,2304]{1,0:T(8,128)(2,1)S(1)} collective-permute-done((bf16[32,2304]{1,0:T(8,128)(2,1)S(1)}, bf16[32,2304]{1,0:T(8,128)(2,1)S(1)}, u32[]{:S(2)}, u32[]{:S(2)}) %collective-permute-start.8) | collective-permute-done | bytes 147488 | tf_op jit(solution)/shard_map/ppermute | solution.py:346
  63.9 1.0 collective-permute-done.10
  64.8 3.3 %collective-permute-done.9 = bf16[32,2304]{1,0:T(8,128)(2,1)S(1)} collective-permute-done((bf16[32,2304]{1,0:T(8,128)(2,1)S(1)}, bf16[32,2304]{1,0:T(8,128)(2,1)S(1)}, u32[]{:S(2)}, u32[]{:S(2)}) %collective-permute-start.9) | collective-permute-done | bytes 147488 | tf_op jit(solution)/shard_map/ppermute | solution.py:346
  68.1 0.1 fusion.1
  68.3 13.3 %all_to_all.21 = bf16[32,2,1152]{2,1,0:T(2,128)(2,1)S(1)} all-to-all(bf16[32,2,1152]{2,1,0:T(2,128)(2,1)S(1)} %reshape.102), channel_id=1, replica_groups=mesh['y'=4,'z'=8,'x'=4,'core'=2] {'y','z'}, dimensions={0} | all-to-all | bytes 294912 | tf_op jit(solution)/shard_map/all_to_all | solution.py:377
  81.6 0.1 share.1
  81.7 21.1 %all_to_all.22 = f32[256,1,128]{2,1,0:T(1,128)S(1)} all-to-all(f32[256,1,128]{2,1,0:T(1,128)S(1)} %bitcast.38), channel_id=1, replica_groups=mesh['y'=4,'z'=8,'x'=4,'core'=2] {'y','z','x','core'}, dimensions={0} | all-to-all | bytes 262144 | tf_op jit(solution)/shard_map/all_to_all | solution.py:379
  102.8 0.0 copy-done.2
  102.8 0.0 copy-done.4
  102.8 0.0 copy-done.6
  102.8 0.0 copy-done.7
  102.8 0.0 copy-done.8
  102.8 0.0 copy-done.9
  102.8 0.0 copy-done.10
  102.8 0.0 copy-done.11
  102.9 0.0 copy-done.12
  102.9 1.0 adam.1
  (11 shorter events, 0.2 us)
Async XLA Ops:
  0.6 37.8 %copy-start = (bf16[2,256,256]{2,1,0:T(8,128)(2,1)S(1)}, bf16[2,256,256]{2,1,0:T(8,128)(2,1)}, u32[]{:S(2)}) copy-start(bf16[2,256,256]{2,1,0:T(8,128)(2,1)} %param.13) | copy-start | bytes 786436
  0.7 0.7 copy-start.1
  1.4 0.7 copy-start.3
  2.1 0.7 copy-start.5
  3.7 21.3 %all-to-all-start = ((bf16[32,2,1152]{2,1,0:T(2,128)(2,1)}), bf16[32,2,1152]{2,1,0:T(2,128)(2,1)S(1)}, u32[]{:S(2)}, u32[]{:S(2)}) async-start(bf16[32,2,1152]{2,1,0:T(2,128)(2,1)} %broadcast_in_dim.19), calls=%async_computation | async-start | bytes 294912 | tf_op jit(solution)/shard_map/all_to_all | solution.py:365
  25.1 6.7 %collective-permute-start.2 = (bf16[32,2304]{1,0:T(8,128)(2,1)S(1)}, bf16[32,2304]{1,0:T(8,128)(2,1)S(1)}, u32[]{:S(2)}, u32[]{:S(2)}) collective-permute-start(bf16[32,2304]{1,0:T(8,128)(2,1)S(1)} %bitcast.30), channel_id=1, source_target_pairs={{0,6},{2,4},{4,2},{6,0},{1,7},{3,5},{5,3},{7,1},{8,14},{10,12},{12... | collective-permute-start | bytes 442376 | tf_op jit(solution)/shard_map/ppermute | solution.py:346
  27.6 7.7 %collective-permute-start.1 = (bf16[32,2304]{1,0:T(8,128)(2,1)S(1)}, bf16[32,2304]{1,0:T(8,128)(2,1)S(1)}, u32[]{:S(2)}, u32[]{:S(2)}) collective-permute-start(bf16[32,2304]{1,0:T(8,128)(2,1)S(1)} %bitcast.31), channel_id=1, source_target_pairs={{0,4},{2,6},{4,0},{6,2},{1,5},{3,7},{5,1},{7,3},{8,12},{10,14},{12... | collective-permute-start | bytes 442376 | tf_op jit(solution)/shard_map/ppermute | solution.py:346
  28.2 8.9 %collective-permute-start = (bf16[32,2304]{1,0:T(8,128)(2,1)S(1)}, bf16[32,2304]{1,0:T(8,128)(2,1)S(1)}, u32[]{:S(2)}, u32[]{:S(2)}) collective-permute-start(bf16[32,2304]{1,0:T(8,128)(2,1)S(1)} %bitcast.32), channel_id=1, source_target_pairs={{0,2},{2,0},{4,6},{6,4},{1,3},{3,1},{5,7},{7,5},{8,10},{10,8},{12,... | collective-permute-start | bytes 442376 | tf_op jit(solution)/shard_map/ppermute | solution.py:346
  28.5 9.4 %collective-permute-start.3 = (bf16[32,2304]{1,0:T(8,128)(2,1)S(1)}, bf16[32,2304]{1,0:T(8,128)(2,1)S(1)}, u32[]{:S(2)}, u32[]{:S(2)}) collective-permute-start(bf16[32,2304]{1,0:T(8,128)(2,1)S(1)} %bitcast.33), channel_id=1, source_target_pairs={{0,1},{1,0},{2,3},{3,2},{4,5},{5,4},{6,7},{7,6},{8,9},{9,8},{10,11... | collective-permute-start | bytes 442376 | tf_op jit(solution)/shard_map/ppermute | solution.py:350
  31.8 6.1 %collective-permute-start.6 = (bf16[32,2304]{1,0:T(8,128)(2,1)S(1)}, bf16[32,2304]{1,0:T(8,128)(2,1)S(1)}, u32[]{:S(2)}, u32[]{:S(2)}) collective-permute-start(bf16[32,2304]{1,0:T(8,128)(2,1)S(1)} %collective-permute-done.2.b3), channel_id=1, source_target_pairs={{0,1},{1,0},{2,3},{3,2},{4,5},{5,4},{6,7},{7,6},{8,9},{9,8},{10,11... | collective-permute-start | bytes 442376 | tf_op jit(solution)/shard_map/ppermute | solution.py:350
  35.3 2.7 %collective-permute-start.5 = (bf16[32,2304]{1,0:T(8,128)(2,1)S(1)}, bf16[32,2304]{1,0:T(8,128)(2,1)S(1)}, u32[]{:S(2)}, u32[]{:S(2)}) collective-permute-start(bf16[32,2304]{1,0:T(8,128)(2,1)S(1)} %collective-permute-done.1.b2), channel_id=1, source_target_pairs={{0,1},{1,0},{2,3},{3,2},{4,5},{5,4},{6,7},{7,6},{8,9},{9,8},{10,11... | collective-permute-start | bytes 442376 | tf_op jit(solution)/shard_map/ppermute | solution.py:350
  37.0 1.4 %collective-permute-start.4 = (bf16[32,2304]{1,0:T(8,128)(2,1)S(1)}, bf16[32,2304]{1,0:T(8,128)(2,1)S(1)}, u32[]{:S(2)}, u32[]{:S(2)}) collective-permute-start(bf16[32,2304]{1,0:T(8,128)(2,1)S(1)} %collective-permute-done.b1), channel_id=1, source_target_pairs={{0,1},{1,0},{2,3},{3,2},{4,5},{5,4},{6,7},{7,6},{8,9},{9,8},{10,11... | collective-permute-start | bytes 442376 | tf_op jit(solution)/shard_map/ppermute | solution.py:350
  56.2 2.1 %collective-permute-start.7 = (bf16[128,2304]{1,0:T(8,128)(2,1)S(1)}, bf16[128,2304]{1,0:T(8,128)(2,1)S(1)}, u32[]{:S(2)}, u32[]{:S(2)}) collective-permute-start(bf16[128,2304]{1,0:T(8,128)(2,1)S(1)} %get-tuple-element.23), channel_id=1, source_target_pairs={{0,1},{1,0},{2,3},{3,2},{4,5},{5,4},{6,7},{7,6},{8,9},{9,8},{10,11... | collective-permute-start | bytes 1769480 | tf_op jit(solution)/shard_map/ppermute | solution.py:350
  58.5 44.3 %copy-start.2 = (f32[1024]{0:T(1024)S(1)}, f32[1024]{0:T(1024)}, u32[]{:S(2)}) copy-start(f32[1024]{0:T(1024)} %param.17) | copy-start | bytes 12292
  58.5 44.3 %copy-start.4 = (f32[1024]{0:T(1024)S(1)}, f32[1024]{0:T(1024)}, u32[]{:S(2)}) copy-start(f32[1024]{0:T(1024)} %param.18) | copy-start | bytes 12292
  58.5 44.3 %copy-start.6 = (f32[256]{0:T(256)S(1)}, f32[256]{0:T(256)}, u32[]{:S(2)}) copy-start(f32[256]{0:T(256)} %param.19) | copy-start | bytes 3076
  58.5 44.3 %copy-start.7 = (f32[1024]{0:T(1024)S(1)}, f32[1024]{0:T(1024)}, u32[]{:S(2)}) copy-start(f32[1024]{0:T(1024)} %param.20) | copy-start | bytes 12292
  58.5 44.3 %copy-start.8 = (f32[1024]{0:T(1024)S(1)}, f32[1024]{0:T(1024)}, u32[]{:S(2)}) copy-start(f32[1024]{0:T(1024)} %param.21) | copy-start | bytes 12292
  58.5 44.3 %copy-start.9 = (f32[1024]{0:T(1024)S(1)}, f32[1024]{0:T(1024)}, u32[]{:S(2)}) copy-start(f32[1024]{0:T(1024)} %param.23) | copy-start | bytes 12292
  58.6 44.3 %copy-start.10 = (f32[1024]{0:T(1024)S(1)}, f32[1024]{0:T(1024)}, u32[]{:S(2)}) copy-start(f32[1024]{0:T(1024)} %param.24) | copy-start | bytes 12292
  58.6 44.3 %copy-start.11 = (f32[256]{0:T(256)S(1)}, f32[256]{0:T(256)}, u32[]{:S(2)}) copy-start(f32[256]{0:T(256)} %param.22) | copy-start | bytes 3076
  58.6 44.3 %copy-start.12 = (f32[256]{0:T(256)S(1)}, f32[256]{0:T(256)}, u32[]{:S(2)}) copy-start(f32[256]{0:T(256)} %param.25) | copy-start | bytes 3076
  58.6 5.3 %collective-permute-start.8 = (bf16[32,2304]{1,0:T(8,128)(2,1)S(1)}, bf16[32,2304]{1,0:T(8,128)(2,1)S(1)}, u32[]{:S(2)}, u32[]{:S(2)}) collective-permute-start(bf16[32,2304]{1,0:T(8,128)(2,1)S(1)} %get-tuple-element.37), channel_id=1, source_target_pairs={{0,2},{2,0},{4,6},{6,4},{1,3},{3,1},{5,7},{7,5},{8,10},{10,8},{12,... | collective-permute-start | bytes 442376 | tf_op jit(solution)/shard_map/ppermute | solution.py:346
  58.9 6.0 %collective-permute-start.10 = (bf16[32,2304]{1,0:T(8,128)(2,1)S(1)}, bf16[32,2304]{1,0:T(8,128)(2,1)S(1)}, u32[]{:S(2)}, u32[]{:S(2)}) collective-permute-start(bf16[32,2304]{1,0:T(8,128)(2,1)S(1)} %get-tuple-element.38), channel_id=1, source_target_pairs={{0,6},{2,4},{4,2},{6,0},{1,7},{3,5},{5,3},{7,1},{8,14},{10,12},{12... | collective-permute-start | bytes 442376 | tf_op jit(solution)/shard_map/ppermute | solution.py:346
  60.7 7.4 %collective-permute-start.9 = (bf16[32,2304]{1,0:T(8,128)(2,1)S(1)}, bf16[32,2304]{1,0:T(8,128)(2,1)S(1)}, u32[]{:S(2)}, u32[]{:S(2)}) collective-permute-start(bf16[32,2304]{1,0:T(8,128)(2,1)S(1)} %get-tuple-element.39), channel_id=1, source_target_pairs={{0,4},{2,6},{4,0},{6,2},{1,5},{3,7},{5,1},{7,3},{8,12},{10,14},{12... | collective-permute-start | bytes 442376 | tf_op jit(solution)/shard_map/ppermute | solution.py:346
